TPU v7x, 32 devices: a 4x2x2 block of a 4x4x8 slice. The times are simulated.
32 devices in a mesh: dp: 4 (over y, z), tp: 8 (over x, core).
Axes of the slice: x: 4, y: 2, z: 2, core: 2. Of those that a mesh axis runs over, the one named last changes fastest.
The devices are a block of a 4x4x8 slice.
Arguments:
- tokens: int32 [4, 512], P('dp'), parts along dimension 0
- positions: int32 [4, 512], P('dp'), parts along dimension 0
- embed_table: bfloat16 [128256, 3072], P('tp')
- w_query: bfloat16 [3072, 24, 128], P(None, 'tp')
- w_key: bfloat16 [3072, 8, 128], P(None, 'tp')
- w_value: bfloat16 [3072, 8, 128], P(None, 'tp')
- w_out: bfloat16 [24, 128, 3072], P('tp')
- w_gate: bfloat16 [3072, 8192], P(None, 'tp')
- w_up: bfloat16 [3072, 8192], P(None, 'tp')
- w_down: bfloat16 [8192, 3072], P('tp')
- norm_pre_att: float32 [3072], replicated
- norm_post_att: float32 [3072], replicated
- norm_pre_ffw: float32 [3072], replicated
- norm_post_ffw: float32 [3072], replicated
Outputs:
- output: bfloat16 [4, 512, 3072], P('dp', 'tp'), parts along dimension 0
There are 4 independent parts. A program takes and returns all parts, laid end to end along the dimension named above; an argument that names none is the same for every part.
All inputs are finite; a program needn't handle non-finite values.
Results may differ from a plain program's by a relative error of at most 0.02.
Values are sent between devices in bfloat16 or wider.
A program may use at most 768 MiB of HBM per device.

v0:
```python
import jax
import jax.numpy as jnp
from jax import lax
from jax.sharding import PartitionSpec as P

WINDOW = 4096
QUERY_SCALE = 256.0 ** -0.5
SOFT_CAP = 50.0
NORM_EPS = 1e-6
ROPE_BASE = 10000.0


def rms_norm(hidden, norm_scale):
    hidden = hidden.astype(jnp.float32)
    mean_sq = jnp.mean(hidden * hidden, axis=-1, keepdims=True)
    return (hidden * lax.rsqrt(mean_sq + NORM_EPS) * (1.0 + norm_scale)).astype(jnp.bfloat16)


def rope_tables(positions, head_dim):
    half_dim = head_dim // 2
    inv_freq = ROPE_BASE ** (-2.0 * jnp.arange(half_dim, dtype=jnp.float32) / head_dim)
    angles = positions.astype(jnp.float32)[:, :, None] * inv_freq
    return jnp.cos(angles)[:, :, None, :], jnp.sin(angles)[:, :, None, :]


def apply_rope(states, cos_tab, sin_tab):
    half_dim = states.shape[-1] // 2
    lower_half = states[..., :half_dim]
    upper_half = states[..., half_dim:]
    return jnp.concatenate([lower_half * cos_tab - upper_half * sin_tab, upper_half * cos_tab + lower_half * sin_tab], axis=-1)


def local_attention(q_states, k_states, v_states, positions):
    seq_len = q_states.shape[1]
    q_block = min(128, seq_len)
    key_span = min(seq_len, WINDOW + q_block)

    def one_block(block_idx):
        q_start = block_idx * q_block
        k_start = jnp.maximum(q_start + q_block - key_span, 0)
        q_blk = lax.dynamic_slice_in_dim(q_states, q_start, q_block, axis=1)
        k_blk = lax.dynamic_slice_in_dim(k_states, k_start, key_span, axis=1)
        v_blk = lax.dynamic_slice_in_dim(v_states, k_start, key_span, axis=1)
        q_pos = lax.dynamic_slice_in_dim(positions, q_start, q_block, axis=1)
        k_pos = lax.dynamic_slice_in_dim(positions, k_start, key_span, axis=1)
        scores = jnp.einsum("bqkgd,blkd->bkgql", q_blk, k_blk, preferred_element_type=jnp.float32)
        capped = SOFT_CAP * jnp.tanh(scores / SOFT_CAP)
        offset = q_pos[:, :, None] - k_pos[:, None, :]
        keep_mask = (offset >= 0) & (offset < WINDOW)
        capped = jnp.where(keep_mask[:, None, None, :, :], capped, -1e30)
        att_probs = jax.nn.softmax(capped, axis=-1).astype(jnp.bfloat16)
        att_mix = jnp.einsum("bkgql,blkd->bqkgd", att_probs, v_blk, preferred_element_type=jnp.float32)
        return att_mix.astype(jnp.bfloat16)

    blocks = lax.map(one_block, jnp.arange(seq_len // q_block))
    return jnp.moveaxis(blocks, 0, 1).reshape(q_states.shape)


def decoder_layer(embeds, positions, w_query, w_key, w_value, w_out, w_gate, w_up, w_down, norm_pre_att, norm_post_att, norm_pre_ffw, norm_post_ffw):
    n_batch, seq_len = positions.shape
    model_dim = embeds.shape[-1]
    kv_local, head_dim = w_key.shape[1], w_key.shape[2]
    n_group = w_query.shape[1] // kv_local
    attn_in = lax.all_gather(rms_norm(embeds, norm_pre_att), "tp", axis=1, tiled=True)
    cos_tab, sin_tab = rope_tables(positions, head_dim)
    q_proj = jnp.einsum("bsd,dnh->bsnh", attn_in, w_query, preferred_element_type=jnp.float32)
    q_states = (apply_rope(q_proj, cos_tab, sin_tab) * QUERY_SCALE).astype(jnp.bfloat16)
    q_states = q_states.reshape(n_batch, seq_len, kv_local, n_group, head_dim)
    k_proj = jnp.einsum("bsd,dnh->bsnh", attn_in, w_key, preferred_element_type=jnp.float32)
    k_states = apply_rope(k_proj, cos_tab, sin_tab).astype(jnp.bfloat16)
    v_states = jnp.einsum("bsd,dnh->bsnh", attn_in, w_value, preferred_element_type=jnp.float32).astype(jnp.bfloat16)
    att_mix = local_attention(q_states, k_states, v_states, positions)
    w_out_grp = w_out.reshape(kv_local, n_group, head_dim, model_dim)
    att_part = jnp.einsum("bskgh,kghd->bsd", att_mix, w_out_grp, preferred_element_type=jnp.float32).astype(jnp.bfloat16)
    att_proj = lax.psum_scatter(att_part, "tp", scatter_dimension=1, tiled=True)
    resid_one = (embeds.astype(jnp.float32) + rms_norm(att_proj, norm_post_att).astype(jnp.float32)).astype(jnp.bfloat16)
    mlp_in = lax.all_gather(rms_norm(resid_one, norm_pre_ffw), "tp", axis=1, tiled=True)
    gate_pre = jnp.einsum("bsd,df->bsf", mlp_in, w_gate, preferred_element_type=jnp.float32)
    up_proj = jnp.einsum("bsd,df->bsf", mlp_in, w_up, preferred_element_type=jnp.float32)
    ffn_act = (jax.nn.gelu(gate_pre, approximate=True) * up_proj).astype(jnp.bfloat16)
    down_part = jnp.einsum("bsf,fd->bsd", ffn_act, w_down, preferred_element_type=jnp.float32).astype(jnp.bfloat16)
    down_proj = lax.psum_scatter(down_part, "tp", scatter_dimension=1, tiled=True)
    return (resid_one.astype(jnp.float32) + rms_norm(down_proj, norm_post_ffw).astype(jnp.float32)).astype(jnp.bfloat16)


def solution(mesh):
    in_specs = (P("dp", None), P("dp", None), P("tp", None), P(None, "tp", None), P(None, "tp", None), P(None, "tp", None), P("tp", None, None), P(None, "tp"), P(None, "tp"), P("tp", None), P(None), P(None), P(None), P(None))

    def device_step(tokens, positions, embed_block, w_query, w_key, w_value, w_out, w_gate, w_up, w_down, norm_pre_att, norm_post_att, norm_pre_ffw, norm_post_ffw):
        dev_rank = lax.axis_index("tp")
        vocab_local, model_dim = embed_block.shape
        local_ids = tokens - dev_rank * vocab_local
        in_block = (local_ids >= 0) & (local_ids < vocab_local)
        looked = jnp.take(embed_block, jnp.clip(local_ids, 0, vocab_local - 1), axis=0)
        normalizer = jnp.sqrt(jnp.float32(model_dim)).astype(jnp.bfloat16)
        partial_emb = jnp.where(in_block[:, :, None], looked * normalizer, jnp.zeros((), jnp.bfloat16))
        embeds = lax.psum_scatter(partial_emb, "tp", scatter_dimension=1, tiled=True)
        return decoder_layer(embeds, positions, w_query, w_key, w_value, w_out, w_gate, w_up, w_down, norm_pre_att, norm_post_att, norm_pre_ffw, norm_post_ffw)

    return jax.shard_map(device_step, mesh=mesh, in_specs=in_specs, out_specs=P("dp", "tp", None), check_vma=False)
```

profile of v0, /device:TPU:81, one launch (start us, length us, event | category | flops | bytes accessed | tf_op | source)
XLA Modules:
  0.0 248.0 jit_solution(12438902711429252869)
XLA Ops:
  6.6 0.9 and_reduce_fusion
  7.4 16.4 %gather_fusion = bf16[512,3072]{1,0:T(8,128)(2,1)} fusion(bf16[16032,3072]{1,0:T(8,128)(2,1)} %param.18, s32[1024]{0:T(1024)S(1)} %pad_clamp_fusion), kind=kCustom, calls=%fused_computation | custom fusion | bytes 6293504 | tf_op jit(solution)/shard_map/jit(_take)/gather | solution.py:94
  23.8 4.2 %fusion.28 = bf16[1,512,3072]{2,1,0:T(8,128)(2,1)} fusion(bf16[512,3072]{1,0:T(8,128)(2,1)} %gather_fusion, pred[512]{0:T(512)(128)(4,1)S(1)} %get-tuple-element.73, pred[512]{0:T(512)(128)(4,1)S(1)} %get-tuple-element.83), kind=kLoop, calls=%fused_computation.39 | loop fusion | flops 4718592 | bytes 6292480 | tf_op jit(solution)/shard_map/jit(_where)/select_n | solution.py:96
  28.7 39.9 %reduce-scatter.4.cloned.1.call-done = bf16[1,64,3072]{2,1,0:T(8,128)(2,1)} async-done(((bf16[1,512,3072]{2,1,0:T(8,128)(2,1)}), bf16[1,64,3072]{2,1,0:T(8,128)(2,1)}) %reduce-scatter.4.cloned.1.call-update) | async-done | bytes 393232 | tf_op jit(solution)/shard_map/reduce_scatter | solution.py:97
  68.6 1.2 fusion.55
  69.8 2.0 fusion.57
  71.9 4.3 %copy.18 = bf16[3072,3,128]{0,2,1:T(8,128)(2,1)} copy(bf16[3072,3,128]{2,0,1:T(8,128)(2,1)} %param.19) | data formatting | bytes 4718592 | tf_op args[3]
  76.8 22.0 %all-gather.3.cloned.1.call-done = bf16[1,512,3072]{2,1,0:T(8,128)(2,1)} async-done(((bf16[1,64,3072]{2,1,0:T(8,128)(2,1)}), bf16[1,512,3072]{2,1,0:T(8,128)(2,1)}) %all-gather.3.cloned.1.call-update) | async-done | bytes 3145744 | tf_op jit(solution)/shard_map/all_gather | solution.py:64
  98.8 3.0 %fusion.40 = f32[1,512,1,128]{1,3,2,0:T(8,128)S(1)} fusion(bf16[1,512,3072]{2,1,0:T(8,128)(2,1)} %all-gather.3.cloned.1.call-done, bf16[3072,1,128]{2,0,1:T(8,128)(2,1)S(1)} %copy-done.3), kind=kOutput, calls=%fused_computation.56 | convolution fusion | flops 402653184 | bytes 4194304 | tf_op jit(solution)/shard_map/bsd,dnh->bsnh/dot_general | solution.py:69
  102.6 4.2 %fusion.25 = f32[512,384]{0,1:S(1)} fusion(bf16[3072,384]{0,1:T(8,128)(2,1)} %bitcast.124, bf16[1,512,3072]{2,1,0:T(8,128)(2,1)} %all-gather.3.cloned.1.call-done), kind=kOutput, calls=%fused_computation.35 | convolution fusion | flops 1207959552 | bytes 6291456
  107.0 1.0 fusion.46
  107.9 13.0 %while.10 = (s32[]{:T(128)}, bf16[4,1,128,1,3,128]{5,2,0,4,3,1:T(8,128)(2,1)}, s32[4]{0:T(128)S(1)}, s32[1,512]{1,0:T(1,128)S(1)}, bf16[1,512,1,3,128]{1,4,3,2,0...) while((s32[]{:T(128)}, ...), condition=%wide.region_5.6_spmd, body=%wide.region_2.5_spmd.sunk | while | flops 102743296 | bytes 2961071 | solution.py:55
  108.0 0.7 dynamic_slice.29
  110.2 1.0 fusion.101
  111.2 0.7 dynamic_slice.29
  113.4 1.0 fusion.101
  114.4 0.7 dynamic_slice.29
  116.7 1.0 fusion.101
  117.7 0.7 dynamic_slice.29
  119.9 1.0 fusion.101
  120.9 4.3 %fusion.16 = bf16[1,512,3072]{2,1,0:T(8,128)(2,1)} fusion(bf16[512,3,128]{2,0,1:T(8,128)(2,1)} %bitcast.130, bf16[3,128,3072]{2,1,0:T(8,128)(2,1)S(1)} %copy-done), kind=kOutput, calls=%fused_computation.26 | convolution fusion | flops 1209532416 | bytes 5898240 | tf_op jit(solution)/shard_map/bskgh,kghd->bsd/dot_general | solution.py:74
  125.4 29.4 %reduce-scatter.6.cloned.1.call-done = bf16[1,64,3072]{2,1,0:T(8,128)(2,1)} async-done(((bf16[1,512,3072]{2,1,0:T(8,128)(2,1)}), bf16[1,64,3072]{2,1,0:T(8,128)(2,1)}) %reduce-scatter.6.cloned.1.call-update) | async-done | bytes 393232 | tf_op jit(solution)/shard_map/reduce_scatter | solution.py:75
  154.8 1.2 fusion.49
  156.0 1.4 fusion.59
  157.3 0.9 fusion.61
  158.6 26.7 %all-gather.5.cloned.1.call-done = bf16[1,512,3072]{2,1,0:T(8,128)(2,1)} async-done(((bf16[1,64,3072]{2,1,0:T(8,128)(2,1)}), bf16[1,512,3072]{2,1,0:T(8,128)(2,1)}) %all-gather.5.cloned.1.call-update) | async-done | bytes 3145744 | tf_op jit(solution)/shard_map/all_gather | solution.py:77
  185.2 8.5 %fusion.19 = f32[512,1024]{1,0:T(8,128)} fusion(bf16[3072,1024]{1,0:T(8,128)(2,1)} %param.23, bf16[1,512,3072]{2,1,0:T(8,128)(2,1)} %all-gather.5.cloned.1.call-done), kind=kOutput, calls=%fused_computation.29 | convolution fusion | flops 3221225472 | bytes 11534336 | tf_op jit(solution)/shard_map/bsd,df->bsf/dot_general | solution.py:78
  193.7 14.9 %fusion.15 = bf16[1,512,3072]{2,1,0:T(8,128)(2,1)} fusion(bf16[1024,3072]{1,0:T(8,128)(2,1)} %param.25, f32[512,1024]{1,0:T(8,128)} %fusion.19, bf16[3072,1024]{1,0:T(8,128)(2,1)} %param.24, bf16[1,512,3072]{2,1,0:T(8,128)(2,1)} %all-gather.5.cloned.1.call-done), kind=kOutput, calls=%fused_computation.25 | convolution fusion | flops 6449266688 | bytes 20971520 | tf_op jit(solution)/shard_map/bsf,fd->bsd/dot_general | solution.py:81
  208.7 0.6 copy-done.9
  209.4 28.9 %reduce-scatter.8.cloned.1.call-done = bf16[1,64,3072]{2,1,0:T(8,128)(2,1)} async-done(((bf16[1,512,3072]{2,1,0:T(8,128)(2,1)}), bf16[1,64,3072]{2,1,0:T(8,128)(2,1)}) %reduce-scatter.8.cloned.1.call-update) | async-done | bytes 393232 | tf_op jit(solution)/shard_map/reduce_scatter | solution.py:82
  238.3 1.2 fusion.52
  239.5 2.0 fusion.62
  (64 shorter events, 6.2 us)
Async XLA Ops:
  6.5 114.4 %copy-start = (bf16[3,128,3072]{2,1,0:T(8,128)(2,1)S(1)}, bf16[3,128,3072]{2,1,0:T(8,128)(2,1)}, u32[]{:S(2)}) copy-start(bf16[3,128,3072]{2,1,0:T(8,128)(2,1)} %param.22) | copy-start | bytes 7077892
  6.6 62.0 %reduce-scatter.4.cloned.1.call-start = ((), (), s32[]{:S(2)}) async-start(), calls=%async_computation.3 | async-start | bytes 3538944 | tf_op jit(solution)/shard_map/reduce_scatter | solution.py:97
  28.0 0.7 copy-start.6
  28.1 70.7 %all-gather.3.cloned.1.call-start = ((), (), s32[]{:S(2)}) async-start(), calls=%async_computation.4 | async-start | bytes 3538944 | tf_op jit(solution)/shard_map/all_gather | solution.py:64
  28.7 47.5 %copy-start.5 = (s32[1,512]{1,0:T(1,128)S(1)}, s32[1,512]{1,0:T(1,128)}, u32[]{:S(2)}) copy-start(s32[1,512]{1,0:T(1,128)} %param.17) | copy-start | bytes 6148
  69.8 29.0 %copy-start.3 = (bf16[3072,1,128]{2,0,1:T(8,128)(2,1)S(1)}, bf16[3072,1,128]{2,0,1:T(8,128)(2,1)}, u32[]{:S(2)}) copy-start(bf16[3072,1,128]{2,0,1:T(8,128)(2,1)} %param.20) | copy-start | bytes 2359300
  71.8 82.9 %reduce-scatter.6.cloned.1.call-start = ((), (), s32[]{:S(2)}) async-start(), calls=%async_computation.5 | async-start | bytes 3538944 | tf_op jit(solution)/shard_map/reduce_scatter | solution.py:75
  102.5 4.4 %copy-start.1 = (bf16[1,512,3072]{2,1,0:T(8,128)(2,1)S(1)}, bf16[1,512,3072]{2,1,0:T(8,128)(2,1)}, u32[]{:S(2)}) copy-start(bf16[1,512,3072]{2,1,0:T(8,128)(2,1)} %all-gather.3.cloned.1.call-done) | copy-start | bytes 9437188
  102.6 4.4 %copy-start.4 = (bf16[3072,1,128]{2,0,1:T(8,128)(2,1)S(1)}, bf16[3072,1,128]{2,0,1:T(8,128)(2,1)}, u32[]{:S(2)}) copy-start(bf16[3072,1,128]{2,0,1:T(8,128)(2,1)} %param.21) | copy-start | bytes 2359300
  120.9 4.4 %copy-start.7 = (f32[3072]{0:T(1024)S(1)}, f32[3072]{0:T(1024)}, u32[]{:S(2)}) copy-start(f32[3072]{0:T(1024)} %param.27) | copy-start | bytes 36868
  120.9 4.4 %copy-start.8 = (f32[3072]{0:T(1024)S(1)}, f32[3072]{0:T(1024)}, u32[]{:S(2)}) copy-start(f32[3072]{0:T(1024)} %param.28) | copy-start | bytes 36868
  125.2 30.8 %copy-start.2 = (bf16[1,64,3072]{2,1,0:T(8,128)(2,1)S(1)}, bf16[1,64,3072]{2,1,0:T(8,128)(2,1)}, u32[]{:S(2)}) copy-start(bf16[1,64,3072]{2,1,0:T(8,128)(2,1)} %reduce-scatter.4.cloned.1.call-done) | copy-start | bytes 1179652
  125.3 60.0 %all-gather.5.cloned.1.call-start = ((), (), s32[]{:S(2)}) async-start(), calls=%async_computation.6 | async-start | bytes 3538944 | tf_op jit(solution)/shard_map/all_gather | solution.py:77
  158.3 80.0 %reduce-scatter.8.cloned.1.call-start = ((), (), s32[]{:S(2)}) async-start(), calls=%async_computation.7 | async-start | bytes 3538944 | tf_op jit(solution)/shard_map/reduce_scatter | solution.py:82
  208.7 0.7 copy-start.9
Sparse Core Ops, SparseCore 0:
  28.2 40.3 reduce-scatter.3
  71.9 26.7 all-gather.2
  125.4 29.3 reduce-scatter.5
  158.4 26.7 all-gather.4
  208.8 29.4 reduce-scatter.7
where the time goes:
time: 250 us; the launch traced here: 248 us
  waiting for transfers between devices  147 us (59%)
  matrix products  41.6 us (17%)
  local copies, waits for them, and re-layouts  24.8 us (10%)
  other arithmetic  17.8 us (7%)
  between operations  13.4 us (5%)
  loops' own time  2.89 us (1%)
    reduce_scatter x1, waiting for transfers between devices, device_step(): lax.psum_scatter(partial_emb, 'tp', scatter_dimension=1, tiled=True)  39.9 us
    reduce_scatter x1, waiting for transfers between devices, decoder_layer(): att_proj = lax.psum_scatter(att_part, 'tp', scatter_dimension=1, tiled=True)  29.4 us
    reduce_scatter x1, waiting for transfers between devices, decoder_layer(): lax.psum_scatter(down_part, 'tp', scatter_dimension=1, tiled=True)  28.9 us
    all_gather x1, waiting for transfers between devices, decoder_layer(): lax.all_gather(rms_norm(resid_one, norm_pre_ffw), 'tp', axis=1, tiled=True)  26.7 us
    all_gather x1, waiting for transfers between devices, decoder_layer(): lax.all_gather(rms_norm(embeds, norm_pre_att), 'tp', axis=1, tiled=True)  22 us
    gather x1, local copies, waits for them, and re-layouts, device_step(): jnp.take(embed_block, jnp.clip(local_ids, 0, vocab_local - 1), axis=0)  16.4 us
    dot_general x1, matrix products, decoder_layer(): jnp.einsum('bsf,fd->bsd', ffn_act, w_down, preferred_element_type=jnp.flo...  14.9 us
    dot_general x1, matrix products, decoder_layer(): jnp.einsum('bsd,df->bsf', mlp_in, w_gate, preferred_element_type=jnp.floa...  8.5 us
  transfers between devices with their start and end apart: 5, of which 5 were waited for; matrix products, arithmetic and copies ran while one was open for 2% of the time, Pallas kernels for 0%

commit v1 on v0

v1 whole, which is shorter than its diff:
```python
import functools

import jax
import jax.numpy as jnp
from jax import lax
from jax.experimental import pallas as pl
from jax.experimental.pallas import tpu as pltpu
from jax.sharding import PartitionSpec as P

WINDOW = 4096
QUERY_SCALE = 256.0 ** -0.5
SOFT_CAP = 50.0
NORM_EPS = 1e-6
ROPE_BASE = 10000.0
MESH = pl.DeviceIdType.MESH
BF16 = jnp.bfloat16
F32 = jnp.float32
PIECES = 4
NT = (((1,), (1,)), ((), ()))


def norm_rows(hidden, scale):
    mean_sq = jnp.mean(hidden * hidden, axis=-1, keepdims=True)
    return (hidden * lax.rsqrt(mean_sq + NORM_EPS) * (1.0 + scale)).astype(BF16)


def layer_kernel(
    n_dev, part_hbm, cos_ref, sin_ref, pcol_ref, prow_ref, wq_hbm, wk_hbm, wv_hbm, wo_hbm, wg_hbm, wu_hbm, wd_hbm,
    g1_ref, g2_ref, g3_ref, g4_ref, out_ref,
    part, wqkv, wo, wg, wu, wd, acts, own, give, take, ring_out, ring_in, q_buf, k_buf, v_buf, o_buf, h_buf, e_own, x_own,
    part_sem, w_sem, ag_s, ag_r, agd_s, agd_r, rs_s, rs_r, rsd_s, rsd_r,
):
    chips = n_dev // 2
    rows = e_own.shape[0]
    piece = rows // PIECES
    dim = e_own.shape[1]
    n_q, head = q_buf.shape[1], q_buf.shape[3]
    ffn = h_buf.shape[1]

    me = lax.axis_index("tp")
    chip, core = lax.div(me, 2), lax.rem(me, 2)
    step = 1 - 2 * core
    partner = {"tp": me + step}
    ahead = {"tp": 2 * lax.rem(chip + step + chips, chips) + core}
    behind = {"tp": 2 * lax.rem(chip - step + chips, chips) + core}

    def mine(s):
        return 2 * lax.rem(chip - step * s + 2 * chips, chips) + core

    def theirs(s):
        return 2 * lax.rem(chip + step * s + 2 * chips, chips) + 1 - core

    def sub(j):
        return pl.ds(pl.multiple_of(j * piece, piece), piece)

    def block_rows(b):
        return pl.ds(pl.multiple_of(b * rows, rows), rows)

    def part_copy(b, i):
        return pltpu.make_async_copy(part_hbm.at[b], part.at[b], part_sem.at[i])

    order = []
    for s in range(chips):
        order.append(theirs(s + 1))
        order.append(mine(s + 1))
    for i, b in enumerate(order):
        part_copy(b, i).start()
    w_copies = [pltpu.make_async_copy(wq_hbm.at[h], wqkv.at[:, pl.ds(h * head, head)], w_sem.at[h]) for h in range(n_q)]
    w_copies.append(pltpu.make_async_copy(wk_hbm, wqkv.at[:, pl.ds(n_q * head, head)], w_sem.at[n_q]))
    w_copies.append(pltpu.make_async_copy(wv_hbm, wqkv.at[:, pl.ds((n_q + 1) * head, head)], w_sem.at[n_q + 1]))
    n_qkv = len(w_copies)
    for i, (src, dst) in enumerate(((wo_hbm, wo), (wg_hbm, wg), (wu_hbm, wu), (wd_hbm, wd))):
        w_copies.append(pltpu.make_async_copy(src, dst, w_sem.at[n_qkv + i]))
    for copy in w_copies:
        copy.start()

    barrier = pltpu.get_barrier_semaphore()
    for peer in (partner, ahead, behind):
        pl.semaphore_signal(barrier, inc=1, device_id=peer, device_id_type=MESH)
    pl.semaphore_wait(barrier, 3)

    def remote(src, dst, send, recv, peer):
        return pltpu.make_async_remote_copy(
            src_ref=src, dst_ref=dst, send_sem=send, recv_sem=recv, device_id=peer, device_id_type=MESH
        )

    def ag_ring(buf, s, j, b):
        return remote(buf.at[b, sub(j)], buf.at[b, sub(j)], ag_s.at[s, j], ag_r.at[s, j], ahead)

    def ag_chip(buf, s, j, b):
        return remote(buf.at[b, sub(j)], buf.at[b, sub(j)], agd_s.at[s, j], agd_r.at[s, j], partner)

    def ag_begin(buf, j):
        ag_ring(buf, 0, j, mine(0)).start()
        ag_chip(buf, 0, j, mine(0)).start()

    def ag_forward(buf, s, j):
        ag_ring(buf, s - 1, j, mine(s)).wait_recv()
        if s < chips - 1:
            ag_ring(buf, s, j, mine(s)).start()
        ag_chip(buf, s, j, mine(s)).start()

    def ag_join(buf, s):
        def body(j, _):
            ag_chip(buf, s, j, theirs(s)).wait_recv()
            return 0
        lax.fori_loop(0, PIECES, body, 0)

    def ag_drain(buf):
        def body(j, _):
            for s in range(chips):
                if s < chips - 1:
                    ag_ring(buf, s, j, mine(s)).wait_send()
                ag_chip(buf, s, j, mine(s)).wait_send()
            return 0
        lax.fori_loop(0, PIECES, body, 0)

    def rs_chip(s, src):
        return remote(src, take.at[s], rsd_s.at[s], rsd_r.at[s], partner)

    def rs_ring(r, t, j):
        slot = (r % 2) * (chips - 1) + t
        return remote(ring_out.at[t, sub(j)], ring_in.at[slot, sub(j)], rs_s.at[t, j], rs_r.at[slot, j], ahead)

    def rs_sum(r, t, j, own_ref):
        s = (t + 1) % chips
        total = own_ref[sub(j), :].astype(F32) + take[s, sub(j), :].astype(F32)
        if t > 0:
            rs_ring(r, t - 1, j).wait_recv()
            total = total + ring_in[(r % 2) * (chips - 1) + t - 1, sub(j), :].astype(F32)
        return total.astype(BF16)

    def rs_stage(r, t, own_ref, src):
        s = (t + 1) % chips
        rs_chip(s, src).wait_recv()

        def body(j, _):
            ring_out[t, sub(j), :] = rs_sum(r, t, j, own_ref)
            rs_ring(r, t, j).start()
            return 0
        lax.fori_loop(0, PIECES, body, 0)

    def rs_last(r, own_ref, src, finish):
        rs_chip(0, src).wait_recv()

        def body(j, _):
            finish(j, rs_sum(r, chips - 1, j, own_ref))
            return 0
        lax.fori_loop(0, PIECES, body, 0)

    def rs_drain(r, src):
        def body(j, _):
            for t in range(chips - 1):
                rs_ring(r, t, j).wait_send()
            return 0
        lax.fori_loop(0, PIECES, body, 0)
        for s in range(chips):
            rs_chip(s, src(s)).wait_send()

    for s in range(chips):
        b = theirs(s + 1)
        part_copy(b, 2 * s).wait()
        rs_chip((s + 1) % chips, part.at[b]).start()
    for s in range(chips):
        part_copy(mine(s + 1), 2 * s + 1).wait()

    def emb_part(s):
        return part.at[theirs(s)]

    for t in range(chips - 1):
        rs_stage(0, t, part.at[mine(t + 1)], emb_part(t + 1))

    def emb_finish(j, e):
        e_own[sub(j), :] = e
        acts[mine(0), sub(j), :] = norm_rows(e.astype(F32), g1_ref[...])
        ag_begin(acts, j)

    rs_last(0, part.at[mine(0)], emb_part(0), emb_finish)
    rs_drain(0, emb_part)

    for copy in w_copies[:n_qkv]:
        copy.wait()

    def pair(ref, s):
        return jnp.concatenate([ref[mine(s)], ref[theirs(s)]], axis=0)

    def pair_rows(ref, s):
        return jnp.concatenate([ref[block_rows(mine(s)), :], ref[block_rows(theirs(s)), :]], axis=0)

    def rope(states, cos, sin):
        return states * cos + pltpu.roll(states, head // 2, axis=1) * sin

    def project(s):
        x = pair(acts, s)
        cos, sin = pair_rows(cos_ref, s), pair_rows(sin_ref, s)
        for start in range(0, n_q + 2, 2):
            width = min(2, n_q + 2 - start)
            res = jnp.dot(x, wqkv[:, start * head : (start + width) * head], preferred_element_type=F32)
            for i in range(width):
                h, states = start + i, res[:, i * head : (i + 1) * head]
                if h < n_q:
                    q_buf[s, h] = (rope(states, cos, sin) * QUERY_SCALE).astype(BF16)
                else:
                    val = (rope(states, cos, sin) if h == n_q else states).astype(BF16)
                    dst = k_buf if h == n_q else v_buf
                    dst[block_rows(mine(s)), :] = val[:rows]
                    dst[block_rows(theirs(s)), :] = val[rows:]

    for s in range(chips):
        if s < chips - 1:
            def body(j, _):
                ag_forward(acts, s + 1, j)
                return 0
        ag_join(acts, s)
        project(s)
        if s < chips - 1:
            lax.fori_loop(0, PIECES, body, 0)

    def attend(s):
        key_pos = prow_ref[...]
        offset = pair_rows(pcol_ref, s) - key_pos
        keep = (offset >= 0) & (offset < WINDOW)

        for h in range(n_q):
            scores = lax.dot_general(q_buf[s, h], k_buf[...], NT, preferred_element_type=F32)
            capped = SOFT_CAP * jnp.tanh(scores * (1.0 / SOFT_CAP))
            weight = jnp.where(keep, jnp.exp(capped), 0.0)
            total = jnp.sum(weight, axis=-1, keepdims=True)
            probs = (weight * (1.0 / total)).astype(BF16)
            mix = jnp.dot(probs, v_buf[...], preferred_element_type=F32)
            o_buf[:, h * head : (h + 1) * head] = mix.astype(BF16)

    def spread(s, lhs_ref, w_ref, width):
        @pl.loop(0, dim // width)
        def _(i):
            cols = pl.ds(pl.multiple_of(i * width, width), width)
            res = jnp.dot(lhs_ref[...], w_ref[:, cols], preferred_element_type=F32).astype(BF16)
            own[s, :, cols] = res[:rows]
            give[s, :, cols] = res[rows:]
        rs_chip(s, give.at[s]).start()

    w_copies[n_qkv].wait()
    for i in range(chips):
        s = (i + 1) % chips
        attend(s)
        spread(s, o_buf, wo, 512)
        if i > 0:
            rs_stage(1, i - 1, own.at[i], give.at[i])
    ag_drain(acts)

    def att_finish(j, y):
        x1 = (e_own[sub(j), :].astype(F32) + norm_rows(y.astype(F32), g2_ref[...]).astype(F32)).astype(BF16)
        x_own[sub(j), :] = x1
        part[mine(0), sub(j), :] = norm_rows(x1.astype(F32), g3_ref[...])
        ag_begin(part, j)

    rs_last(1, own.at[0], give.at[0], att_finish)
    rs_drain(1, lambda s: give.at[s])

    for copy in w_copies[n_qkv + 1 :]:
        copy.wait()
    tile = ffn // PIECES

    def gate_up(s, i):
        x = pair(part, s)
        cols = pl.ds(i * tile, tile)
        gate = jnp.dot(x, wg[:, cols], preferred_element_type=F32)
        up = jnp.dot(x, wu[:, cols], preferred_element_type=F32)
        h_buf[:, cols] = (jax.nn.gelu(gate, approximate=True) * up).astype(BF16)

    for s in range(chips):
        ag_join(part, s)
        if s == chips - 2:
            rs_stage(2, 0, own.at[1], give.at[1])
        for i in range(PIECES):
            gate_up(s, i)
            if s < chips - 1:
                ag_forward(part, s + 1, i)
        spread(s, h_buf, wd, 512)
    for t in range(1, chips - 1):
        rs_stage(2, t, own.at[t + 1], give.at[t + 1])
    ag_drain(part)

    def ffn_finish(j, z):
        out = x_own[sub(j), :].astype(F32) + norm_rows(z.astype(F32), g4_ref[...]).astype(F32)
        out_ref[sub(j), :] = out.astype(BF16)

    rs_last(2, own.at[0], give.at[0], ffn_finish)
    rs_drain(2, lambda s: give.at[s])


def decoder_layer(n_dev, part, positions, w_query, w_key, w_value, w_out, w_gate, w_up, w_down, g1, g2, g3, g4):
    seq_len = positions.shape[1]
    dim, n_q, head = w_query.shape
    ffn = w_gate.shape[1]
    chips, rows = n_dev // 2, seq_len // n_dev
    half = head // 2
    inv_freq = ROPE_BASE ** (-2.0 * jnp.arange(half, dtype=F32) / head)
    angles = positions[0].astype(F32)[:, None] * inv_freq
    cos_tab, sin_tab = jnp.cos(angles), jnp.sin(angles)
    cos2 = jnp.concatenate([cos_tab, cos_tab], axis=1)
    sin2 = jnp.concatenate([-sin_tab, sin_tab], axis=1)
    vmem = pl.BlockSpec(memory_space=pltpu.VMEM)
    hbm = pl.BlockSpec(memory_space=pl.ANY)
    block = (rows, dim)
    dma = pltpu.SemaphoreType.DMA
    return pl.pallas_call(
        functools.partial(layer_kernel, n_dev),
        name="layer",
        out_shape=jax.ShapeDtypeStruct((rows, dim), BF16),
        in_specs=[hbm] + [vmem] * 4 + [hbm] * 7 + [vmem] * 4,
        out_specs=vmem,
        scratch_shapes=[
            pltpu.VMEM((n_dev,) + block, BF16),
            pltpu.VMEM((dim, (n_q + 2) * head), BF16),
            pltpu.VMEM((n_q * head, dim), BF16),
            pltpu.VMEM((dim, ffn), BF16),
            pltpu.VMEM((dim, ffn), BF16),
            pltpu.VMEM((ffn, dim), BF16),
            pltpu.VMEM((n_dev,) + block, BF16),
            pltpu.VMEM((chips,) + block, BF16),
            pltpu.VMEM((chips,) + block, BF16),
            pltpu.VMEM((chips,) + block, BF16),
            pltpu.VMEM((chips - 1,) + block, BF16),
            pltpu.VMEM((2 * (chips - 1),) + block, BF16),
            pltpu.VMEM((chips, n_q, 2 * rows, head), BF16),
            pltpu.VMEM((seq_len, head), BF16),
            pltpu.VMEM((seq_len, head), BF16),
            pltpu.VMEM((2 * rows, n_q * head), BF16),
            pltpu.VMEM((2 * rows, ffn), BF16),
            pltpu.VMEM(block, BF16),
            pltpu.VMEM(block, BF16),
            dma((n_dev,)),
            dma((n_q + 6,)),
            dma((chips - 1, PIECES)),
            dma((chips - 1, PIECES)),
            dma((chips, PIECES)),
            dma((chips, PIECES)),
            dma((chips - 1, PIECES)),
            dma((2 * (chips - 1), PIECES)),
            dma((chips,)),
            dma((chips,)),
        ],
        compiler_params=pltpu.CompilerParams(collective_id=0, has_side_effects=True, vmem_limit_bytes=58 * 1024 * 1024),
    )(
        part.reshape((n_dev,) + block), cos2, sin2, positions.reshape(seq_len, 1), positions.reshape(1, seq_len),
        w_query.transpose(1, 0, 2), w_key.reshape(dim, head), w_value.reshape(dim, head), w_out.reshape(n_q * head, dim),
        w_gate, w_up, w_down, g1.reshape(1, dim), g2.reshape(1, dim), g3.reshape(1, dim), g4.reshape(1, dim),
    )


def solution(mesh):
    n_dev = mesh.shape["tp"]
    in_specs = (P("dp", None), P("dp", None), P("tp", None), P(None, "tp", None), P(None, "tp", None), P(None, "tp", None), P("tp", None, None), P(None, "tp"), P(None, "tp"), P("tp", None), P(None), P(None), P(None), P(None))

    def device_step(tokens, positions, embed_block, *weights):
        dev_rank = lax.axis_index("tp")
        vocab_local, model_dim = embed_block.shape
        local_ids = tokens[0] - dev_rank * vocab_local
        in_block = (local_ids >= 0) & (local_ids < vocab_local)
        looked = jnp.take(embed_block, jnp.clip(local_ids, 0, vocab_local - 1), axis=0)
        normalizer = jnp.sqrt(jnp.float32(model_dim)).astype(BF16)
        part = jnp.where(in_block[:, None], looked * normalizer, jnp.zeros((), BF16))
        return decoder_layer(n_dev, part, positions, *weights)[None]

    return jax.shard_map(device_step, mesh=mesh, in_specs=in_specs, out_specs=P("dp", "tp", None), check_vma=False)
```

time: 250 us -> 126 us (0.50)
  waiting for transfers between devices: 147 us -> 0 us
  Pallas kernels: 0 us -> 103 us
  matrix products: 41.6 us -> 0 us
  between operations: 13.4 us -> 0.06 us
  other arithmetic: 17.8 us -> 5 us
  local copies, waits for them, and re-layouts: 24.8 us -> 18.2 us
  loops' own time: 2.89 us -> 0 us
    pallas_call x0 -> x1, Pallas kernels: none -> 103 us  [decoder_layer(): pl.pallas_call(functools.partial(layer_kernel, n_dev), name='layer', out_...]
    reduce_scatter x3 -> x0, waiting for transfers between devices: 98.2 us -> none  [the longest x1 39.9 us: device_step(): lax.psum_scatter(partial_emb, 'tp', scatter_dimension=1, tiled=True)]
    all_gather x2 -> x0, waiting for transfers between devices: 48.7 us -> none  [the longest x1 26.7 us: decoder_layer(): lax.all_gather(rms_norm(resid_one, norm_pre_ffw), 'tp', axis=1, tiled=True)]
    dot_general x13 -> x0, matrix products: 37.4 us -> none  [the longest x1 14.9 us: decoder_layer(): jnp.einsum('bsf,fd->bsd', ffn_act, w_down, preferred_element_type=jnp.flo...]
    reduce_sum x8 -> x0, other arithmetic: 6.05 us -> none  [the longest x4 4.88 us: rms_norm(): mean_sq = jnp.mean(hidden * hidden, axis=-1, keepdims=True)]
    convert_element_type x5 -> x1, other arithmetic: 4.91 us -> 0.01 us  [decoder_layer(): angles = positions[0].astype(F32)[:, None] * inv_freq]
    unnamed x1 -> x0, matrix products: 4.18 us -> none
    unnamed x21 -> x5, local copies, waits for them, and re-layouts: 5.54 us -> 1.78 us
  transfers between devices with their start and end apart: 5 -> 0, of which waited for: 5 -> 0; matrix products, arithmetic and copies ran while one was open for 2% -> 0% of each run, Pallas kernels for 0% -> 0%
where the time goes in v1:
time: 126 us
  Pallas kernels  103 us (82%)
  local copies, waits for them, and re-layouts  18.2 us (14%)
  other arithmetic  5 us (4%)
    pallas_call x1, Pallas kernels, decoder_layer(): pl.pallas_call(functools.partial(layer_kernel, n_dev), name='layer', out_...  103 us
    gather x1, local copies, waits for them, and re-layouts, device_step(): jnp.take(embed_block, jnp.clip(local_ids, 0, vocab_local - 1), axis=0)  15.4 us

profile of v1, /device:TPU:81, one launch (start us, length us, event | category | flops | bytes accessed | tf_op | source)
XLA Modules:
  0.0 126.0 jit_solution(16953931926243341917)
XLA Ops:
  0.0 0.7 compare_select_fusion
  0.7 0.0 copy-start.1
  0.7 15.4 %gather_fusion = bf16[512,3072]{1,0:T(8,128)(2,1)S(1)} fusion(bf16[16032,3072]{1,0:T(8,128)(2,1)} %param.16, s32[1024]{0:T(1024)S(1)} %pad_clamp_fusion), kind=kCustom, calls=%fused_computation | custom fusion | bytes 6293504 | tf_op jit(solution)/shard_map/jit(_take)/gather | solution.py:361
  16.2 0.0 copy-done.1
  16.2 0.1 min.16
  16.3 0.1 and.20
  16.4 0.0 copy-start
  16.4 2.3 %multiply_select_fusion.part_hbm = bf16[8,64,3072]{2,1,0:T(8,128)(2,1)} fusion(bf16[8,64,3072]{2,1,0:T(8,128)(2,1)S(1)} %bitcast.15, pred[8,64]{1,0:T(8,128)(4,1)S(1)} %compare_and_fusion, pred[8,64]{1,0:T(8,128)(4,1)S(1)} %and.20), kind=kLoop, calls=%fused_computation.1 | loop fusion | flops 4718592 | bytes 6292480 | tf_op jit(solution)/shard_map/jit(_where)/select_n | solution.py:363
  18.7 0.0 copy-done
  18.7 1.0 fusion
  19.7 1.0 pad_maximum_fusion
  20.7 0.8 copy.15.pcol_ref
  21.5 102.7 %layer.1 = bf16[64,3072]{1,0:T(8,128)(2,1)} custom-call(bf16[8,64,3072]{2,1,0:T(8,128)(2,1)} %multiply_select_fusion.part_hbm, f32[512,128]{1,0:T(8,128)} %get-tuple-element.8.cos_ref, f32[512,128]{1,0:T(8,128)} %get-tuple-element.9.sin_ref, s32[512,1]{1,0:T(8,128)} %copy.15.pcol_ref, s32[1,512]{1,0:T(1,128)} %prow_ref.1, bf16[3,3072,128]{2,1,0:T(8,128)(2,1)} %bitcast.16, ...), custom_call_target="tpu_custom_call" | custom-call | tf_op jit(solution)/shard_map/layer/pallas_call | solution.py:307
  124.3 1.8 %copy.17 = bf16[1,64,3072]{2,1,0:T(8,128)(2,1)} copy(bf16[1,64,3072]{2,1,0:T(8,128)(2,1)} %bitcast.18) | data formatting | bytes 786432
  (6 shorter events, 0.1 us)
Async XLA Ops:
  0.7 15.5 %copy-start.1 = (s32[1,512]{1,0:T(1,128)S(1)}, s32[1,512]{1,0:T(1,128)}, u32[]{:S(2)}) copy-start(s32[1,512]{1,0:T(1,128)} %param.14) | copy-start | bytes 6148
  16.4 2.3 %copy-start = (s32[1,512]{1,0:T(1,128)S(1)}, s32[1,512]{1,0:T(1,128)}, u32[]{:S(2)}) copy-start(s32[1,512]{1,0:T(1,128)} %prow_ref.1) | copy-start | bytes 6148

commit v2 on v1

--- a/solution.py
+++ b/solution.py
@@ -16,6 +16,8 @@
 BF16 = jnp.bfloat16
 F32 = jnp.float32
 PIECES = 4
+TOKENS = 128
+UNROLL = 8
 NT = (((1,), (1,)), ((), ()))
 
 
@@ -25,10 +27,10 @@
 
 
 def layer_kernel(
-    n_dev, part_hbm, cos_ref, sin_ref, pcol_ref, prow_ref, wq_hbm, wk_hbm, wv_hbm, wo_hbm, wg_hbm, wu_hbm, wd_hbm,
+    n_dev, part, freq_ref, prow_ref, wq_hbm, wk_hbm, wv_hbm, wo_hbm, wg_hbm, wu_hbm, wd_hbm,
     g1_ref, g2_ref, g3_ref, g4_ref, out_ref,
-    part, wqkv, wo, wg, wu, wd, acts, own, give, take, ring_out, ring_in, q_buf, k_buf, v_buf, o_buf, h_buf, e_own, x_own,
-    part_sem, w_sem, ag_s, ag_r, agd_s, agd_r, rs_s, rs_r, rsd_s, rsd_r,
+    wqkv, wo, wg, wu, wd, acts, acts2, cos_ref, sin_ref, pcol_ref, own, give, take, ring_out, ring_in, q_buf, k_buf, v_buf, o_buf, h_buf, e_own, x_own,
+    w_sem, ag_s, ag_r, agd_s, agd_r, rs_s, rs_r, rsd_s, rsd_r,
 ):
     chips = n_dev // 2
     rows = e_own.shape[0]
@@ -56,15 +58,6 @@
     def block_rows(b):
         return pl.ds(pl.multiple_of(b * rows, rows), rows)
 
-    def part_copy(b, i):
-        return pltpu.make_async_copy(part_hbm.at[b], part.at[b], part_sem.at[i])
-
-    order = []
-    for s in range(chips):
-        order.append(theirs(s + 1))
-        order.append(mine(s + 1))
-    for i, b in enumerate(order):
-        part_copy(b, i).start()
     w_copies = [pltpu.make_async_copy(wq_hbm.at[h], wqkv.at[:, pl.ds(h * head, head)], w_sem.at[h]) for h in range(n_q)]
     w_copies.append(pltpu.make_async_copy(wk_hbm, wqkv.at[:, pl.ds(n_q * head, head)], w_sem.at[n_q]))
     w_copies.append(pltpu.make_async_copy(wv_hbm, wqkv.at[:, pl.ds((n_q + 1) * head, head)], w_sem.at[n_q + 1]))
@@ -157,18 +150,20 @@
         for s in range(chips):
             rs_chip(s, src(s)).wait_send()
 
-    for s in range(chips):
-        b = theirs(s + 1)
-        part_copy(b, 2 * s).wait()
-        rs_chip((s + 1) % chips, part.at[b]).start()
-    for s in range(chips):
-        part_copy(mine(s + 1), 2 * s + 1).wait()
-
     def emb_part(s):
         return part.at[theirs(s)]
 
+    for s in range(chips):
+        rs_chip((s + 1) % chips, emb_part(s + 1)).start()
     for t in range(chips - 1):
         rs_stage(0, t, part.at[mine(t + 1)], emb_part(t + 1))
+        if t == 0:
+            pcol_ref[...] = jnp.transpose(jnp.broadcast_to(prow_ref[...], (head, prow_ref.shape[1])))
+            angles = pcol_ref[...].astype(F32) * freq_ref[...]
+            lane = lax.broadcasted_iota(jnp.int32, angles.shape, 1)
+            cos_ref[...] = jnp.cos(angles)
+            sin = jnp.sin(angles)
+            sin_ref[...] = jnp.where(lane < head // 2, -sin, sin)
 
     def emb_finish(j, e):
         e_own[sub(j), :] = e
@@ -218,7 +213,7 @@
 
     def attend(s):
         key_pos = prow_ref[...]
-        offset = pair_rows(pcol_ref, s) - key_pos
+        offset = pair_rows(pcol_ref, s)[:, 0:1] - key_pos
         keep = (offset >= 0) & (offset < WINDOW)
 
         for h in range(n_q):
@@ -251,8 +246,8 @@
     def att_finish(j, y):
         x1 = (e_own[sub(j), :].astype(F32) + norm_rows(y.astype(F32), g2_ref[...]).astype(F32)).astype(BF16)
         x_own[sub(j), :] = x1
-        part[mine(0), sub(j), :] = norm_rows(x1.astype(F32), g3_ref[...])
-        ag_begin(part, j)
+        acts2[mine(0), sub(j), :] = norm_rows(x1.astype(F32), g3_ref[...])
+        ag_begin(acts2, j)
 
     rs_last(1, own.at[0], give.at[0], att_finish)
     rs_drain(1, lambda s: give.at[s])
@@ -262,24 +257,24 @@
     tile = ffn // PIECES
 
     def gate_up(s, i):
-        x = pair(part, s)
+        x = pair(acts2, s)
         cols = pl.ds(i * tile, tile)
         gate = jnp.dot(x, wg[:, cols], preferred_element_type=F32)
         up = jnp.dot(x, wu[:, cols], preferred_element_type=F32)
         h_buf[:, cols] = (jax.nn.gelu(gate, approximate=True) * up).astype(BF16)
 
     for s in range(chips):
-        ag_join(part, s)
+        ag_join(acts2, s)
         if s == chips - 2:
             rs_stage(2, 0, own.at[1], give.at[1])
         for i in range(PIECES):
             gate_up(s, i)
             if s < chips - 1:
-                ag_forward(part, s + 1, i)
+                ag_forward(acts2, s + 1, i)
         spread(s, h_buf, wd, 512)
     for t in range(1, chips - 1):
         rs_stage(2, t, own.at[t + 1], give.at[t + 1])
-    ag_drain(part)
+    ag_drain(acts2)
 
     def ffn_finish(j, z):
         out = x_own[sub(j), :].astype(F32) + norm_rows(z.astype(F32), g4_ref[...]).astype(F32)
@@ -287,6 +282,82 @@
 
     rs_last(2, own.at[0], give.at[0], ffn_finish)
     rs_drain(2, lambda s: give.at[s])
+
+
+def lookup_kernel(n_dev, tok_ref, tokrow_ref, table_hbm, out_ref, slots, tokcol, counts, sem):
+    vocab, dim = table_hbm.shape
+    seq_len = out_ref.shape[0]
+    base = lax.axis_index("tp") * vocab
+    n_blocks = seq_len // TOKENS
+    unit = 8
+
+    for g in range(n_blocks):
+        def issue(i, count):
+            for u in range(UNROLL):
+                local = tok_ref[0, g * TOKENS + i * UNROLL + u] - base
+                inside = (local >= 0) & (local < vocab)
+
+                @pl.when(inside)
+                def _():
+                    src = pl.multiple_of(lax.shift_left(lax.shift_right_logical(local, 3), 3), unit)
+                    dst = pl.multiple_of((g * TOKENS + count) * unit, unit)
+                    pltpu.make_async_copy(table_hbm.at[pl.ds(src, unit), :], slots.at[pl.ds(dst, unit), :], sem.at[g]).start()
+                count = count + jnp.where(inside, 1, 0)
+            return count
+        counts[g] = lax.fori_loop(0, TOKENS // UNROLL, issue, jnp.int32(0))
+
+    tokcol[...] = jnp.transpose(jnp.broadcast_to(tokrow_ref[...], (TOKENS, seq_len)))
+    scale = jnp.sqrt(jnp.float32(dim)).astype(BF16).astype(F32)
+    depth = 256
+    before = lax.broadcasted_iota(jnp.int32, (TOKENS, TOKENS), 1) < lax.broadcasted_iota(jnp.int32, (TOKENS, TOKENS), 0)
+    col = lax.broadcasted_iota(jnp.int32, (TOKENS, depth), 1)
+    slot_row = lax.broadcasted_iota(jnp.int32, (depth, dim), 0)
+
+    for g in range(n_blocks):
+        count = counts[g]
+
+        def wait(i, _):
+            pltpu.make_async_copy(table_hbm.at[pl.ds(0, unit), :], slots.at[pl.ds(0, unit), :], sem.at[g]).wait()
+            return 0
+        lax.fori_loop(0, count, wait, 0)
+        span = slice(g * TOKENS, (g + 1) * TOKENS)
+        row = tokrow_ref[:, span] - base
+        row_in = ((row >= 0) & (row < vocab)).astype(F32)
+        place = jnp.sum(jnp.where(before, row_in, 0.0), axis=1, keepdims=True).astype(jnp.int32)
+        local = tokcol[span, 0:1] - base
+        inside = (local >= 0) & (local < vocab)
+        want = jnp.where(inside, place * unit + (local & 7), -1)
+
+        def pick(kt):
+            first = pl.multiple_of((g * TOKENS * unit) + kt * depth, depth)
+            hot = (col + kt * depth == want).astype(F32).astype(BF16)
+            held = jnp.where(slot_row + kt * depth < count * unit, slots[pl.ds(first, depth), :], jnp.zeros((), BF16))
+            return (jnp.dot(hot, held, preferred_element_type=F32) * scale).astype(BF16)
+
+        out_ref[span, :] = pick(0)
+
+        def more(kt, _):
+            out_ref[span, :] = out_ref[span, :] + pick(kt)
+            return 0
+        lax.fori_loop(1, lax.div(count * unit + depth - 1, depth), more, 0)
+
+
+def lookup(n_dev, tokens, embed_block):
+    seq_len, dim = tokens.shape[1], embed_block.shape[1]
+    return pl.pallas_call(
+        functools.partial(lookup_kernel, n_dev),
+        name="lookup",
+        out_shape=jax.ShapeDtypeStruct((seq_len, dim), BF16),
+        in_specs=[pl.BlockSpec(memory_space=pltpu.SMEM), pl.BlockSpec(memory_space=pltpu.VMEM), pl.BlockSpec(memory_space=pl.ANY)],
+        out_specs=pl.BlockSpec(memory_space=pltpu.VMEM),
+        scratch_shapes=[
+            pltpu.VMEM((8 * seq_len, dim), BF16),
+            pltpu.VMEM((seq_len, TOKENS), jnp.int32),
+            pltpu.SMEM((seq_len // TOKENS,), jnp.int32),
+            pltpu.SemaphoreType.DMA((seq_len // TOKENS,)),
+        ],
+        compiler_params=pltpu.CompilerParams(vmem_limit_bytes=48 * 1024 * 1024),
+    )(tokens, tokens, embed_block)
 
 
 def decoder_layer(n_dev, part, positions, w_query, w_key, w_value, w_out, w_gate, w_up, w_down, g1, g2, g3, g4):
@@ -294,30 +365,34 @@
     dim, n_q, head = w_query.shape
     ffn = w_gate.shape[1]
     chips, rows = n_dev // 2, seq_len // n_dev
-    half = head // 2
-    inv_freq = ROPE_BASE ** (-2.0 * jnp.arange(half, dtype=F32) / head)
-    angles = positions[0].astype(F32)[:, None] * inv_freq
-    cos_tab, sin_tab = jnp.cos(angles), jnp.sin(angles)
-    cos2 = jnp.concatenate([cos_tab, cos_tab], axis=1)
-    sin2 = jnp.concatenate([-sin_tab, sin_tab], axis=1)
+    inv_freq = ROPE_BASE ** (-2.0 * jnp.arange(head // 2, dtype=F32) / head)
+    freq = jnp.concatenate([inv_freq, inv_freq])[None, :]
     vmem = pl.BlockSpec(memory_space=pltpu.VMEM)
-    hbm = pl.BlockSpec(memory_space=pl.ANY)
+    hbm = pl.BlockSpec(memory_space=pltpu.HBM)
     block = (rows, dim)
     dma = pltpu.SemaphoreType.DMA
+    weights = (
+        w_query.transpose(1, 0, 2), w_key.reshape(dim, head), w_value.reshape(dim, head), w_out.reshape(n_q * head, dim),
+        w_gate, w_up, w_down,
+    )
+    weights = [pltpu.with_memory_space_constraint(w, pltpu.HBM) for w in weights]
     return pl.pallas_call(
         functools.partial(layer_kernel, n_dev),
         name="layer",
         out_shape=jax.ShapeDtypeStruct((rows, dim), BF16),
-        in_specs=[hbm] + [vmem] * 4 + [hbm] * 7 + [vmem] * 4,
+        in_specs=[vmem] * 3 + [hbm] * 7 + [vmem] * 4,
         out_specs=vmem,
         scratch_shapes=[
-            pltpu.VMEM((n_dev,) + block, BF16),
             pltpu.VMEM((dim, (n_q + 2) * head), BF16),
             pltpu.VMEM((n_q * head, dim), BF16),
             pltpu.VMEM((dim, ffn), BF16),
             pltpu.VMEM((dim, ffn), BF16),
             pltpu.VMEM((ffn, dim), BF16),
             pltpu.VMEM((n_dev,) + block, BF16),
+            pltpu.VMEM((n_dev,) + block, BF16),
+            pltpu.VMEM((seq_len, head), F32),
+            pltpu.VMEM((seq_len, head), F32),
+            pltpu.VMEM((seq_len, head), jnp.int32),
             pltpu.VMEM((chips,) + block, BF16),
             pltpu.VMEM((chips,) + block, BF16),
             pltpu.VMEM((chips,) + block, BF16),
@@ -330,7 +405,6 @@
             pltpu.VMEM((2 * rows, ffn), BF16),
             pltpu.VMEM(block, BF16),
             pltpu.VMEM(block, BF16),
-            dma((n_dev,)),
             dma((n_q + 6,)),
             dma((chips - 1, PIECES)),
             dma((chips - 1, PIECES)),
@@ -341,11 +415,9 @@
             dma((chips,)),
             dma((chips,)),
         ],
-        compiler_params=pltpu.CompilerParams(collective_id=0, has_side_effects=True, vmem_limit_bytes=58 * 1024 * 1024),
+        compiler_params=pltpu.CompilerParams(collective_id=0, has_side_effects=True, vmem_limit_bytes=46 * 1024 * 1024),
     )(
-        part.reshape((n_dev,) + block), cos2, sin2, positions.reshape(seq_len, 1), positions.reshape(1, seq_len),
-        w_query.transpose(1, 0, 2), w_key.reshape(dim, head), w_value.reshape(dim, head), w_out.reshape(n_q * head, dim),
-        w_gate, w_up, w_down, g1.reshape(1, dim), g2.reshape(1, dim), g3.reshape(1, dim), g4.reshape(1, dim),
+        pltpu.with_memory_space_constraint(part.reshape((n_dev,) + block), pltpu.VMEM), freq, positions, *weights, g1.reshape(1, dim), g2.reshape(1, dim), g3.reshape(1, dim), g4.reshape(1, dim),
     )
 
 
@@ -354,13 +426,7 @@
     in_specs = (P("dp", None), P("dp", None), P("tp", None), P(None, "tp", None), P(None, "tp", None), P(None, "tp", None), P("tp", None, None), P(None, "tp"), P(None, "tp"), P("tp", None), P(None), P(None), P(None), P(None))
 
     def device_step(tokens, positions, embed_block, *weights):
-        dev_rank = lax.axis_index("tp")
-        vocab_local, model_dim = embed_block.shape
-        local_ids = tokens[0] - dev_rank * vocab_local
-        in_block = (local_ids >= 0) & (local_ids < vocab_local)
-        looked = jnp.take(embed_block, jnp.clip(local_ids, 0, vocab_local - 1), axis=0)
-        normalizer = jnp.sqrt(jnp.float32(model_dim)).astype(BF16)
-        part = jnp.where(in_block[:, None], looked * normalizer, jnp.zeros((), BF16))
+        part = lookup(n_dev, tokens, embed_block)
         return decoder_layer(n_dev, part, positions, *weights)[None]
 
     return jax.shard_map(device_step, mesh=mesh, in_specs=in_specs, out_specs=P("dp", "tp", None), check_vma=False)

time: 126 us -> 99 us (0.79)
  local copies, waits for them, and re-layouts: 18.2 us -> 1.46 us
  Pallas kernels: 103 us -> 97.3 us
  other arithmetic: 5 us -> 0.09 us
    gather x1 -> x0, local copies, waits for them, and re-layouts: 15.4 us -> none  [device_step(): jnp.take(embed_block, jnp.clip(local_ids, 0, vocab_local - 1), axis=0)]
    pallas_call x1, Pallas kernels: 103 us -> 88.2 us  [decoder_layer(): pl.pallas_call(functools.partial(layer_kernel, n_dev), name='layer', out_...]
    pallas_call x0 -> x1, Pallas kernels: none -> 9.08 us  [lookup(): pl.pallas_call(functools.partial(lookup_kernel, n_dev), name='lookup', ou...]
    select_n x2 -> x0, other arithmetic: 2.96 us -> none  [the longest x1 2.27 us: device_step(): jnp.where(in_block[:, None], looked * normalizer, jnp.zeros((), BF16))]
where the time goes in v2:
time: 99 us; the launch traced here: 98.9 us
  Pallas kernels  97.3 us (98%)
  local copies, waits for them, and re-layouts  1.46 us (1%)
    pallas_call x1, Pallas kernels, decoder_layer(): pl.pallas_call(functools.partial(layer_kernel, n_dev), name='layer', out_...  88.2 us
    pallas_call x1, Pallas kernels, lookup(): pl.pallas_call(functools.partial(lookup_kernel, n_dev), name='lookup', ou...  9.08 us

profile of v2, /device:TPU:81, one launch (start us, length us, event | category | flops | bytes accessed | tf_op | source)
XLA Modules:
  0.0 98.9 jit_solution(5015450572347353876)
XLA Ops:
  0.0 0.1 maximum_bitcast_fusion.freq_ref
  0.1 0.0 copy-start.4
  0.1 0.7 copy-done.4
  0.8 0.0 copy-start
  0.8 0.0 copy-start.1
  0.8 0.0 copy-start.2
  0.8 0.0 copy-start.3
  0.8 0.0 copy-start.5
  0.8 9.1 %lookup.1 = bf16[512,3072]{1,0:T(8,128)(2,1)S(1)} custom-call(s32[1,512]{1,0:T(1,128)S(1)} %copy-done.4, s32[1,512]{1,0:T(1,128)S(1)} %copy-done.4, bf16[16032,3072]{1,0:T(8,128)(2,1)} %table_hbm.1), custom_call_target="tpu_custom_call" | custom-call | tf_op jit(solution)/shard_map/lookup/pallas_call | solution.py:347
  9.9 0.0 copy-done
  9.9 0.0 copy-done.1
  9.9 0.0 copy-done.2
  9.9 0.0 copy-done.3
  9.9 0.0 copy-done.5
  9.9 88.2 %layer.1 = bf16[64,3072]{1,0:T(8,128)(2,1)S(1)} custom-call(bf16[8,64,3072]{2,1,0:T(8,128)(2,1)S(1)} %bitcast.12, f32[1,128]{1,0:T(1,128)S(1)} %maximum_bitcast_fusion.freq_ref, s32[1,512]{1,0:T(1,128)S(1)} %copy-done.5, bf16[3,3072,128]{2,1,0:T(8,128)(2,1)} %bitcast.18, bf16[3072,128]{1,0:T(8,128)(2,1)} %bitcast.20, bf16[3072,128]{1,0:T(8,128)(2,1)} %bitcast.21, ...), custom_call_target="tpu_custom_call" | custom-call | tf_op jit(solution)/shard_map/layer/pallas_call | solution.py:379
  98.2 0.7 copy.16
  (1 shorter events, 0.0 us)
Async XLA Ops:
  0.1 0.7 copy-start.4
  0.8 9.1 %copy-start = (f32[3072]{0:T(1024)S(1)}, f32[3072]{0:T(1024)}, u32[]{:S(2)}) copy-start(f32[3072]{0:T(1024)} %param.24) | copy-start | bytes 36868
  0.8 9.1 %copy-start.1 = (f32[3072]{0:T(1024)S(1)}, f32[3072]{0:T(1024)}, u32[]{:S(2)}) copy-start(f32[3072]{0:T(1024)} %param.25) | copy-start | bytes 36868
  0.8 9.1 %copy-start.2 = (f32[3072]{0:T(1024)S(1)}, f32[3072]{0:T(1024)}, u32[]{:S(2)}) copy-start(f32[3072]{0:T(1024)} %param.26) | copy-start | bytes 36868
  0.8 9.1 %copy-start.3 = (f32[3072]{0:T(1024)S(1)}, f32[3072]{0:T(1024)}, u32[]{:S(2)}) copy-start(f32[3072]{0:T(1024)} %param.27) | copy-start | bytes 36868
  0.8 9.1 %copy-start.5 = (s32[1,512]{1,0:T(1,128)S(1)}, s32[1,512]{1,0:T(1,128)}, u32[]{:S(2)}) copy-start(s32[1,512]{1,0:T(1,128)} %prow_ref.1) | copy-start | bytes 6148

commit v3 on v2

--- a/solution.py
+++ b/solution.py
@@ -16,6 +16,8 @@
 BF16 = jnp.bfloat16
 F32 = jnp.float32
 PIECES = 4
+SPREAD = 3072
+FFN_TILE = 512
 TOKENS = 128
 UNROLL = 8
 NT = (((1,), (1,)), ((), ()))
@@ -108,8 +110,17 @@
             return 0
         lax.fori_loop(0, PIECES, body, 0)
 
-    def rs_chip(s, src):
-        return remote(src, take.at[s], rsd_s.at[s], rsd_r.at[s], partner)
+    def rs_chip_rows(s, j, b):
+        return remote(part.at[b, sub(j)], take.at[s, sub(j)], rsd_s.at[s, j], rsd_r.at[s, j], partner)
+
+    def rs_chip_cols(s, i):
+        return remote(give.at[s], take.at[s], rsd_s.at[s, i], rsd_r.at[s, i], partner)
+
+    def cols_arrive(s):
+        def body(i, _):
+            rs_chip_cols(s, i).wait_recv()
+            return 0
+        lax.fori_loop(0, 1, body, 0)
 
     def rs_ring(r, t, j):
         slot = (r % 2) * (chips - 1) + t
@@ -123,55 +134,81 @@
             total = total + ring_in[(r % 2) * (chips - 1) + t - 1, sub(j), :].astype(F32)
         return total.astype(BF16)
 
-    def rs_stage(r, t, own_ref, src):
-        s = (t + 1) % chips
-        rs_chip(s, src).wait_recv()
-
-        def body(j, _):
-            ring_out[t, sub(j), :] = rs_sum(r, t, j, own_ref)
-            rs_ring(r, t, j).start()
-            return 0
-        lax.fori_loop(0, PIECES, body, 0)
-
-    def rs_last(r, own_ref, src, finish):
-        rs_chip(0, src).wait_recv()
-
-        def body(j, _):
-            finish(j, rs_sum(r, chips - 1, j, own_ref))
-            return 0
-        lax.fori_loop(0, PIECES, body, 0)
-
-    def rs_drain(r, src):
+    def rs_piece(r, t, own_ref, j):
+        ring_out[t, sub(j), :] = rs_sum(r, t, j, own_ref)
+        rs_ring(r, t, j).start()
+
+    def rs_stage(r, t):
+        cols_arrive(t + 1)
+
+        def body(j, _):
+            rs_piece(r, t, own.at[t + 1], j)
+            return 0
+        lax.fori_loop(0, PIECES, body, 0)
+
+    def rs_last(r, finish):
+        cols_arrive(0)
+
+        def body(j, _):
+            finish(j, rs_sum(r, chips - 1, j, own.at[0]))
+            return 0
+        lax.fori_loop(0, PIECES, body, 0)
+
+    def ring_drain(r):
         def body(j, _):
             for t in range(chips - 1):
                 rs_ring(r, t, j).wait_send()
             return 0
         lax.fori_loop(0, PIECES, body, 0)
-        for s in range(chips):
-            rs_chip(s, src(s)).wait_send()
-
-    def emb_part(s):
-        return part.at[theirs(s)]
+
+    def cols_drain():
+        def body(i, _):
+            for s in range(chips):
+                rs_chip_cols(s, i).wait_send()
+            return 0
+        lax.fori_loop(0, 1, body, 0)
+
+    seq_len = prow_ref.shape[1]
+    table_rows = seq_len // ((chips - 2) * PIECES)
+    pcol_ref[...] = jnp.transpose(jnp.broadcast_to(prow_ref[...], (head, seq_len)))
+
+    def rotary(i):
+        span = pl.ds(pl.multiple_of(i * table_rows, table_rows), table_rows)
+        angles = pcol_ref[span, :].astype(F32) * freq_ref[...]
+        lane = lax.broadcasted_iota(jnp.int32, angles.shape, 1)
+        cos_ref[span, :] = jnp.cos(angles)
+        sin = jnp.sin(angles)
+        sin_ref[span, :] = jnp.where(lane < head // 2, -sin, sin)
 
     for s in range(chips):
-        rs_chip((s + 1) % chips, emb_part(s + 1)).start()
+        def body(j, _):
+            rs_chip_rows((s + 1) % chips, j, theirs(s + 1)).start()
+            return 0
+        lax.fori_loop(0, PIECES, body, 0)
     for t in range(chips - 1):
-        rs_stage(0, t, part.at[mine(t + 1)], emb_part(t + 1))
-        if t == 0:
-            pcol_ref[...] = jnp.transpose(jnp.broadcast_to(prow_ref[...], (head, prow_ref.shape[1])))
-            angles = pcol_ref[...].astype(F32) * freq_ref[...]
-            lane = lax.broadcasted_iota(jnp.int32, angles.shape, 1)
-            cos_ref[...] = jnp.cos(angles)
-            sin = jnp.sin(angles)
-            sin_ref[...] = jnp.where(lane < head // 2, -sin, sin)
-
-    def emb_finish(j, e):
+        def body(j, _):
+            rs_chip_rows(t + 1, j, theirs(t + 1)).wait_recv()
+            rs_piece(0, t, part.at[mine(t + 1)], j)
+            if t < chips - 2:
+                rotary(t * PIECES + j)
+            return 0
+        lax.fori_loop(0, PIECES, body, 0)
+
+    def emb_finish(j, _):
+        rs_chip_rows(0, j, theirs(0)).wait_recv()
+        e = rs_sum(0, chips - 1, j, part.at[mine(0)])
         e_own[sub(j), :] = e
         acts[mine(0), sub(j), :] = norm_rows(e.astype(F32), g1_ref[...])
         ag_begin(acts, j)
-
-    rs_last(0, part.at[mine(0)], emb_part(0), emb_finish)
-    rs_drain(0, emb_part)
+        return 0
+    lax.fori_loop(0, PIECES, emb_finish, 0)
+    ring_drain(0)
+
+    def emb_drain(j, _):
+        for s in range(chips):
+            rs_chip_rows(s, j, theirs(s)).wait_send()
+        return 0
+    lax.fori_loop(0, PIECES, emb_drain, 0)
 
     for copy in w_copies[:n_qkv]:
         copy.wait()
@@ -225,22 +262,24 @@
             mix = jnp.dot(probs, v_buf[...], preferred_element_type=F32)
             o_buf[:, h * head : (h + 1) * head] = mix.astype(BF16)
 
-    def spread(s, lhs_ref, w_ref, width):
-        @pl.loop(0, dim // width)
+    def spread(s, lhs_ref, w_ref):
+        @pl.loop(0, dim // SPREAD)
         def _(i):
-            cols = pl.ds(pl.multiple_of(i * width, width), width)
+            cols = pl.ds(pl.multiple_of(i * SPREAD, SPREAD), SPREAD)
             res = jnp.dot(lhs_ref[...], w_ref[:, cols], preferred_element_type=F32).astype(BF16)
+            give[s, :, cols] = res[rows:]
             own[s, :, cols] = res[:rows]
-            give[s, :, cols] = res[rows:]
-        rs_chip(s, give.at[s]).start()
+        rs_chip_cols(s, 0).start()
 
     w_copies[n_qkv].wait()
     for i in range(chips):
         s = (i + 1) % chips
         attend(s)
-        spread(s, o_buf, wo, 512)
-        if i > 0:
-            rs_stage(1, i - 1, own.at[i], give.at[i])
+        if i == 1:
+            rs_stage(1, 0)
+        spread(s, o_buf, wo)
+    for t in range(1, chips - 1):
+        rs_stage(1, t)
     ag_drain(acts)
 
     def att_finish(j, y):
@@ -249,16 +288,18 @@
         acts2[mine(0), sub(j), :] = norm_rows(x1.astype(F32), g3_ref[...])
         ag_begin(acts2, j)
 
-    rs_last(1, own.at[0], give.at[0], att_finish)
-    rs_drain(1, lambda s: give.at[s])
+    rs_last(1, att_finish)
+    ring_drain(1)
+    cols_drain()
 
     for copy in w_copies[n_qkv + 1 :]:
         copy.wait()
-    tile = ffn // PIECES
+    n_tiles = ffn // FFN_TILE
+    per_tile = PIECES // n_tiles
 
     def gate_up(s, i):
         x = pair(acts2, s)
-        cols = pl.ds(i * tile, tile)
+        cols = pl.ds(i * FFN_TILE, FFN_TILE)
         gate = jnp.dot(x, wg[:, cols], preferred_element_type=F32)
         up = jnp.dot(x, wu[:, cols], preferred_element_type=F32)
         h_buf[:, cols] = (jax.nn.gelu(gate, approximate=True) * up).astype(BF16)
@@ -266,22 +307,24 @@
     for s in range(chips):
         ag_join(acts2, s)
         if s == chips - 2:
-            rs_stage(2, 0, own.at[1], give.at[1])
-        for i in range(PIECES):
+            rs_stage(2, 0)
+        for i in range(n_tiles):
             gate_up(s, i)
             if s < chips - 1:
-                ag_forward(acts2, s + 1, i)
-        spread(s, h_buf, wd, 512)
+                for j in range(i * per_tile, (i + 1) * per_tile):
+                    ag_forward(acts2, s + 1, j)
+        spread(s, h_buf, wd)
     for t in range(1, chips - 1):
-        rs_stage(2, t, own.at[t + 1], give.at[t + 1])
+        rs_stage(2, t)
     ag_drain(acts2)
 
     def ffn_finish(j, z):
         out = x_own[sub(j), :].astype(F32) + norm_rows(z.astype(F32), g4_ref[...]).astype(F32)
         out_ref[sub(j), :] = out.astype(BF16)
 
-    rs_last(2, own.at[0], give.at[0], ffn_finish)
-    rs_drain(2, lambda s: give.at[s])
+    rs_last(2, ffn_finish)
+    ring_drain(2)
+    cols_drain()
 
 
 def lookup_kernel(n_dev, tok_ref, tokrow_ref, table_hbm, out_ref, slots, tokcol, counts, sem):
@@ -408,12 +451,12 @@
             dma((n_q + 6,)),
             dma((chips - 1, PIECES)),
             dma((chips - 1, PIECES)),
-            dma((chips, PIECES)),
-            dma((chips, PIECES)),
+            dma((chips, 8)),
+            dma((chips, 8)),
             dma((chips - 1, PIECES)),
             dma((2 * (chips - 1), PIECES)),
-            dma((chips,)),
-            dma((chips,)),
+            dma((chips, 8)),
+            dma((chips, 8)),
         ],
         compiler_params=pltpu.CompilerParams(collective_id=0, has_side_effects=True, vmem_limit_bytes=46 * 1024 * 1024),
     )(

time: 99 us -> 93.2 us (0.941)
  Pallas kernels: 97.3 us -> 91.5 us
    pallas_call x1, Pallas kernels: 88.2 us -> 82.5 us  [decoder_layer(): pl.pallas_call(functools.partial(layer_kernel, n_dev), name='layer', out_...]
where the time goes in v3:
time: 93.2 us; the launch traced here: 93.1 us
  Pallas kernels  91.5 us (98%)
  local copies, waits for them, and re-layouts  1.46 us (2%)
    pallas_call x1, Pallas kernels, decoder_layer(): pl.pallas_call(functools.partial(layer_kernel, n_dev), name='layer', out_...  82.5 us
    pallas_call x1, Pallas kernels, lookup(): pl.pallas_call(functools.partial(lookup_kernel, n_dev), name='lookup', ou...  8.93 us

profile of v3, /device:TPU:81, one launch (start us, length us, event | category | flops | bytes accessed | tf_op | source)
XLA Modules:
  0.0 93.1 jit_solution(17381493745247250826)
XLA Ops:
  0.0 0.1 maximum_bitcast_fusion.freq_ref
  0.1 0.0 copy-start.4
  0.1 0.7 copy-done.4
  0.8 0.0 copy-start
  0.8 0.0 copy-start.1
  0.8 0.0 copy-start.2
  0.8 0.0 copy-start.3
  0.8 0.0 copy-start.5
  0.8 8.9 %lookup.1 = bf16[512,3072]{1,0:T(8,128)(2,1)S(1)} custom-call(s32[1,512]{1,0:T(1,128)S(1)} %copy-done.4, s32[1,512]{1,0:T(1,128)S(1)} %copy-done.4, bf16[16032,3072]{1,0:T(8,128)(2,1)} %table_hbm.1), custom_call_target="tpu_custom_call" | custom-call | tf_op jit(solution)/shard_map/lookup/pallas_call | solution.py:390
  9.7 0.0 copy-done
  9.7 0.0 copy-done.1
  9.8 0.0 copy-done.2
  9.8 0.0 copy-done.3
  9.8 0.0 copy-done.5
  9.8 82.5 %layer.1 = bf16[64,3072]{1,0:T(8,128)(2,1)S(1)} custom-call(bf16[8,64,3072]{2,1,0:T(8,128)(2,1)S(1)} %bitcast.12, f32[1,128]{1,0:T(1,128)S(1)} %maximum_bitcast_fusion.freq_ref, s32[1,512]{1,0:T(1,128)S(1)} %copy-done.5, bf16[3,3072,128]{2,1,0:T(8,128)(2,1)} %bitcast.18, bf16[3072,128]{1,0:T(8,128)(2,1)} %bitcast.20, bf16[3072,128]{1,0:T(8,128)(2,1)} %bitcast.21, ...), custom_call_target="tpu_custom_call" | custom-call | tf_op jit(solution)/shard_map/layer/pallas_call | solution.py:422
  92.3 0.7 copy.16
  (1 shorter events, 0.0 us)
Async XLA Ops:
  0.1 0.7 copy-start.4
  0.8 9.0 %copy-start = (f32[3072]{0:T(1024)S(1)}, f32[3072]{0:T(1024)}, u32[]{:S(2)}) copy-start(f32[3072]{0:T(1024)} %param.24) | copy-start | bytes 36868
  0.8 9.0 %copy-start.1 = (f32[3072]{0:T(1024)S(1)}, f32[3072]{0:T(1024)}, u32[]{:S(2)}) copy-start(f32[3072]{0:T(1024)} %param.25) | copy-start | bytes 36868
  0.8 9.0 %copy-start.2 = (f32[3072]{0:T(1024)S(1)}, f32[3072]{0:T(1024)}, u32[]{:S(2)}) copy-start(f32[3072]{0:T(1024)} %param.26) | copy-start | bytes 36868
  0.8 9.0 %copy-start.3 = (f32[3072]{0:T(1024)S(1)}, f32[3072]{0:T(1024)}, u32[]{:S(2)}) copy-start(f32[3072]{0:T(1024)} %param.27) | copy-start | bytes 36868
  0.8 9.0 %copy-start.5 = (s32[1,512]{1,0:T(1,128)S(1)}, s32[1,512]{1,0:T(1,128)}, u32[]{:S(2)}) copy-start(s32[1,512]{1,0:T(1,128)} %prow_ref.1) | copy-start | bytes 6148

commit v4 on v3

--- a/solution.py
+++ b/solution.py
@@ -16,10 +16,8 @@
 BF16 = jnp.bfloat16
 F32 = jnp.float32
 PIECES = 4
-SPREAD = 3072
 FFN_TILE = 512
 TOKENS = 128
-UNROLL = 8
 NT = (((1,), (1,)), ((), ()))
 
 
@@ -113,14 +111,8 @@
     def rs_chip_rows(s, j, b):
         return remote(part.at[b, sub(j)], take.at[s, sub(j)], rsd_s.at[s, j], rsd_r.at[s, j], partner)
 
-    def rs_chip_cols(s, i):
-        return remote(give.at[s], take.at[s], rsd_s.at[s, i], rsd_r.at[s, i], partner)
-
-    def cols_arrive(s):
-        def body(i, _):
-            rs_chip_cols(s, i).wait_recv()
-            return 0
-        lax.fori_loop(0, 1, body, 0)
+    def rs_chip_block(s):
+        return remote(give.at[s], take.at[s], rsd_s.at[s, 0], rsd_r.at[s, 0], partner)
 
     def rs_ring(r, t, j):
         slot = (r % 2) * (chips - 1) + t
@@ -139,7 +131,7 @@
         rs_ring(r, t, j).start()
 
     def rs_stage(r, t):
-        cols_arrive(t + 1)
+        rs_chip_block(t + 1).wait_recv()
 
         def body(j, _):
             rs_piece(r, t, own.at[t + 1], j)
@@ -147,7 +139,7 @@
         lax.fori_loop(0, PIECES, body, 0)
 
     def rs_last(r, finish):
-        cols_arrive(0)
+        rs_chip_block(0).wait_recv()
 
         def body(j, _):
             finish(j, rs_sum(r, chips - 1, j, own.at[0]))
@@ -161,12 +153,9 @@
             return 0
         lax.fori_loop(0, PIECES, body, 0)
 
-    def cols_drain():
-        def body(i, _):
-            for s in range(chips):
-                rs_chip_cols(s, i).wait_send()
-            return 0
-        lax.fori_loop(0, 1, body, 0)
+    def block_drain():
+        for s in range(chips):
+            rs_chip_block(s).wait_send()
 
     seq_len = prow_ref.shape[1]
     table_rows = seq_len // ((chips - 2) * PIECES)
@@ -263,13 +252,10 @@
             o_buf[:, h * head : (h + 1) * head] = mix.astype(BF16)
 
     def spread(s, lhs_ref, w_ref):
-        @pl.loop(0, dim // SPREAD)
-        def _(i):
-            cols = pl.ds(pl.multiple_of(i * SPREAD, SPREAD), SPREAD)
-            res = jnp.dot(lhs_ref[...], w_ref[:, cols], preferred_element_type=F32).astype(BF16)
-            give[s, :, cols] = res[rows:]
-            own[s, :, cols] = res[:rows]
-        rs_chip_cols(s, 0).start()
+        res = jnp.dot(lhs_ref[...], w_ref[...], preferred_element_type=F32).astype(BF16)
+        give[s] = res[rows:]
+        own[s] = res[:rows]
+        rs_chip_block(s).start()
 
     w_copies[n_qkv].wait()
     for i in range(chips):
@@ -290,7 +276,7 @@
 
     rs_last(1, att_finish)
     ring_drain(1)
-    cols_drain()
+    block_drain()
 
     for copy in w_copies[n_qkv + 1 :]:
         copy.wait()
@@ -308,14 +294,17 @@
         ag_join(acts2, s)
         if s == chips - 2:
             rs_stage(2, 0)
+        if s == chips - 1:
+            rs_chip_block(chips - 2).wait_recv()
         for i in range(n_tiles):
             gate_up(s, i)
-            if s < chips - 1:
-                for j in range(i * per_tile, (i + 1) * per_tile):
+            for j in range(i * per_tile, (i + 1) * per_tile):
+                if s < chips - 1:
                     ag_forward(acts2, s + 1, j)
+                else:
+                    rs_piece(2, chips - 3, own.at[chips - 2], j)
         spread(s, h_buf, wd)
-    for t in range(1, chips - 1):
-        rs_stage(2, t)
+    rs_stage(2, chips - 2)
     ag_drain(acts2)
 
     def ffn_finish(j, z):
@@ -324,52 +313,59 @@
 
     rs_last(2, ffn_finish)
     ring_drain(2)
-    cols_drain()
-
-
-def lookup_kernel(n_dev, tok_ref, tokrow_ref, table_hbm, out_ref, slots, tokcol, counts, sem):
+    block_drain()
+
+
+def lookup_kernel(tokrow_ref, table_hbm, out_ref, slots, tokcol, list_v, list_s, list_sem, sem):
     vocab, dim = table_hbm.shape
     seq_len = out_ref.shape[0]
     base = lax.axis_index("tp") * vocab
     n_blocks = seq_len // TOKENS
     unit = 8
-
+    depth = 512
+    square = (TOKENS, TOKENS)
+    lane, line = lax.broadcasted_iota(jnp.int32, square, 1), lax.broadcasted_iota(jnp.int32, square, 0)
+    tokcol[...] = jnp.transpose(jnp.broadcast_to(tokrow_ref[...], (TOKENS, seq_len)))
+
+    wants = []
     for g in range(n_blocks):
-        def issue(i, count):
-            for u in range(UNROLL):
-                local = tok_ref[0, g * TOKENS + i * UNROLL + u] - base
-                inside = (local >= 0) & (local < vocab)
-
-                @pl.when(inside)
-                def _():
-                    src = pl.multiple_of(lax.shift_left(lax.shift_right_logical(local, 3), 3), unit)
-                    dst = pl.multiple_of((g * TOKENS + count) * unit, unit)
-                    pltpu.make_async_copy(table_hbm.at[pl.ds(src, unit), :], slots.at[pl.ds(dst, unit), :], sem.at[g]).start()
-                count = count + jnp.where(inside, 1, 0)
-            return count
-        counts[g] = lax.fori_loop(0, TOKENS // UNROLL, issue, jnp.int32(0))
-
-    tokcol[...] = jnp.transpose(jnp.broadcast_to(tokrow_ref[...], (TOKENS, seq_len)))
-    scale = jnp.sqrt(jnp.float32(dim)).astype(BF16).astype(F32)
-    depth = 256
-    before = lax.broadcasted_iota(jnp.int32, (TOKENS, TOKENS), 1) < lax.broadcasted_iota(jnp.int32, (TOKENS, TOKENS), 0)
-    col = lax.broadcasted_iota(jnp.int32, (TOKENS, depth), 1)
-    slot_row = lax.broadcasted_iota(jnp.int32, (depth, dim), 0)
-
-    for g in range(n_blocks):
-        count = counts[g]
-
-        def wait(i, _):
-            pltpu.make_async_copy(table_hbm.at[pl.ds(0, unit), :], slots.at[pl.ds(0, unit), :], sem.at[g]).wait()
-            return 0
-        lax.fori_loop(0, count, wait, 0)
         span = slice(g * TOKENS, (g + 1) * TOKENS)
         row = tokrow_ref[:, span] - base
         row_in = ((row >= 0) & (row < vocab)).astype(F32)
-        place = jnp.sum(jnp.where(before, row_in, 0.0), axis=1, keepdims=True).astype(jnp.int32)
+        place = jnp.sum(jnp.where(lane < line, row_in, 0.0), axis=1, keepdims=True).astype(jnp.int32)
         local = tokcol[span, 0:1] - base
         inside = (local >= 0) & (local < vocab)
-        want = jnp.where(inside, place * unit + (local & 7), -1)
+        wants.append(jnp.where(inside, place * unit + (local & 7), -1))
+        hits = jnp.where((lane == place) & inside, local.astype(F32), 0.0)
+        list_v[g : g + 1, :] = jnp.sum(hits, axis=0, keepdims=True).astype(jnp.int32)
+        total = jnp.sum(row_in, axis=1, keepdims=True).astype(jnp.int32)
+        list_v[n_blocks + g : n_blocks + g + 1, :] = jnp.broadcast_to(total, (1, TOKENS))
+    to_scalars = pltpu.make_async_copy(list_v, list_s, list_sem)
+    to_scalars.start()
+    to_scalars.wait()
+
+    for g in range(n_blocks):
+        def issue(i, _):
+            local = list_s[g, i]
+            src = pl.multiple_of(lax.shift_left(lax.shift_right_logical(local, 3), 3), unit)
+            dst = pl.multiple_of((g * TOKENS + i) * unit, unit)
+            pltpu.make_async_copy(table_hbm.at[pl.ds(src, unit), :], slots.at[pl.ds(dst, unit), :], sem.at[g]).start()
+            return 0
+        lax.fori_loop(0, list_s[n_blocks + g, 0], issue, 0)
+
+    scale = jnp.sqrt(jnp.float32(dim)).astype(BF16).astype(F32)
+    col = lax.broadcasted_iota(jnp.int32, (TOKENS, depth), 1)
+    slot_row = lax.broadcasted_iota(jnp.int32, (depth, dim), 0)
+
+    for g in range(n_blocks):
+        count = list_s[n_blocks + g, 0]
+        want = wants[g]
+
+        def wait(i, _):
+            pltpu.make_async_copy(table_hbm.at[pl.ds(0, unit), :], slots.at[pl.ds(0, unit), :], sem.at[g]).wait()
+            return 0
+        lax.fori_loop(0, count, wait, 0)
+        span = slice(g * TOKENS, (g + 1) * TOKENS)
 
         def pick(kt):
             first = pl.multiple_of((g * TOKENS * unit) + kt * depth, depth)
@@ -385,22 +381,24 @@
         lax.fori_loop(1, lax.div(count * unit + depth - 1, depth), more, 0)
 
 
-def lookup(n_dev, tokens, embed_block):
+def lookup(tokens, embed_block):
     seq_len, dim = tokens.shape[1], embed_block.shape[1]
     return pl.pallas_call(
-        functools.partial(lookup_kernel, n_dev),
+        lookup_kernel,
         name="lookup",
         out_shape=jax.ShapeDtypeStruct((seq_len, dim), BF16),
-        in_specs=[pl.BlockSpec(memory_space=pltpu.SMEM), pl.BlockSpec(memory_space=pltpu.VMEM), pl.BlockSpec(memory_space=pl.ANY)],
+        in_specs=[pl.BlockSpec(memory_space=pltpu.VMEM), pl.BlockSpec(memory_space=pl.ANY)],
         out_specs=pl.BlockSpec(memory_space=pltpu.VMEM),
         scratch_shapes=[
             pltpu.VMEM((8 * seq_len, dim), BF16),
             pltpu.VMEM((seq_len, TOKENS), jnp.int32),
-            pltpu.SMEM((seq_len // TOKENS,), jnp.int32),
+            pltpu.VMEM((2 * seq_len // TOKENS, TOKENS), jnp.int32),
+            pltpu.SMEM((2 * seq_len // TOKENS, TOKENS), jnp.int32),
+            pltpu.SemaphoreType.DMA,
             pltpu.SemaphoreType.DMA((seq_len // TOKENS,)),
         ],
         compiler_params=pltpu.CompilerParams(vmem_limit_bytes=48 * 1024 * 1024),
-    )(tokens, tokens, embed_block)
+    )(tokens, embed_block)
 
 
 def decoder_layer(n_dev, part, positions, w_query, w_key, w_value, w_out, w_gate, w_up, w_down, g1, g2, g3, g4):
@@ -451,12 +449,12 @@
             dma((n_q + 6,)),
             dma((chips - 1, PIECES)),
             dma((chips - 1, PIECES)),
-            dma((chips, 8)),
-            dma((chips, 8)),
+            dma((chips, PIECES)),
+            dma((chips, PIECES)),
             dma((chips - 1, PIECES)),
             dma((2 * (chips - 1), PIECES)),
-            dma((chips, 8)),
-            dma((chips, 8)),
+            dma((chips, PIECES)),
+            dma((chips, PIECES)),
         ],
         compiler_params=pltpu.CompilerParams(collective_id=0, has_side_effects=True, vmem_limit_bytes=46 * 1024 * 1024),
     )(
@@ -469,7 +467,7 @@
     in_specs = (P("dp", None), P("dp", None), P("tp", None), P(None, "tp", None), P(None, "tp", None), P(None, "tp", None), P("tp", None, None), P(None, "tp"), P(None, "tp"), P("tp", None), P(None), P(None), P(None), P(None))
 
     def device_step(tokens, positions, embed_block, *weights):
-        part = lookup(n_dev, tokens, embed_block)
+        part = lookup(tokens, embed_block)
         return decoder_layer(n_dev, part, positions, *weights)[None]
 
     return jax.shard_map(device_step, mesh=mesh, in_specs=in_specs, out_specs=P("dp", "tp", None), check_vma=False)

time: 93.2 us -> 90.3 us (0.969)
  Pallas kernels: 91.5 us -> 88.2 us
    pallas_call x1, Pallas kernels: 8.93 us -> 6.78 us  [lookup(): pl.pallas_call(lookup_kernel, name='lookup', out_shape=jax.ShapeDtypeStru...]
    pallas_call x1, Pallas kernels: 82.5 us -> 81.4 us  [decoder_layer(): pl.pallas_call(functools.partial(layer_kernel, n_dev), name='layer', out_...]
where the time goes in v4:
time: 90.3 us; the launch traced here: 89.8 us
  Pallas kernels  88.2 us (98%)
  local copies, waits for them, and re-layouts  1.46 us (2%)
    pallas_call x1, Pallas kernels, decoder_layer(): pl.pallas_call(functools.partial(layer_kernel, n_dev), name='layer', out_...  81.4 us
    pallas_call x1, Pallas kernels, lookup(): pl.pallas_call(lookup_kernel, name='lookup', out_shape=jax.ShapeDtypeStru...  6.78 us

profile of v4, /device:TPU:81, one launch (start us, length us, event | category | flops | bytes accessed | tf_op | source)
XLA Modules:
  0.0 89.8 jit_solution(17791978329223107956)
XLA Ops:
  0.0 0.1 maximum_bitcast_fusion.freq_ref
  0.1 0.0 copy-start.4
  0.1 0.7 copy-done.4
  0.8 0.0 copy-start
  0.8 0.0 copy-start.1
  0.8 0.0 copy-start.2
  0.8 0.0 copy-start.3
  0.8 0.0 copy-start.5
  0.8 6.8 %lookup.1 = bf16[512,3072]{1,0:T(8,128)(2,1)S(1)} custom-call(s32[1,512]{1,0:T(1,128)S(1)} %copy-done.4, bf16[16032,3072]{1,0:T(8,128)(2,1)} %table_hbm.1), custom_call_target="tpu_custom_call" | custom-call | tf_op jit(solution)/shard_map/lookup/pallas_call | solution.py:386
  7.6 0.0 copy-done
  7.6 0.0 copy-done.1
  7.6 0.0 copy-done.2
  7.6 0.0 copy-done.3
  7.6 0.0 copy-done.5
  7.6 81.4 %layer.1 = bf16[64,3072]{1,0:T(8,128)(2,1)S(1)} custom-call(bf16[8,64,3072]{2,1,0:T(8,128)(2,1)S(1)} %bitcast.12, f32[1,128]{1,0:T(1,128)S(1)} %maximum_bitcast_fusion.freq_ref, s32[1,512]{1,0:T(1,128)S(1)} %copy-done.5, bf16[3,3072,128]{2,1,0:T(8,128)(2,1)} %bitcast.18, bf16[3072,128]{1,0:T(8,128)(2,1)} %bitcast.20, bf16[3072,128]{1,0:T(8,128)(2,1)} %bitcast.21, ...), custom_call_target="tpu_custom_call" | custom-call | tf_op jit(solution)/shard_map/layer/pallas_call | solution.py:420
  89.1 0.7 copy.16
  (1 shorter events, 0.0 us)
Async XLA Ops:
  0.1 0.7 copy-start.4
  0.8 6.8 %copy-start = (f32[3072]{0:T(1024)S(1)}, f32[3072]{0:T(1024)}, u32[]{:S(2)}) copy-start(f32[3072]{0:T(1024)} %param.24) | copy-start | bytes 36868
  0.8 6.8 %copy-start.1 = (f32[3072]{0:T(1024)S(1)}, f32[3072]{0:T(1024)}, u32[]{:S(2)}) copy-start(f32[3072]{0:T(1024)} %param.25) | copy-start | bytes 36868
  0.8 6.8 %copy-start.2 = (f32[3072]{0:T(1024)S(1)}, f32[3072]{0:T(1024)}, u32[]{:S(2)}) copy-start(f32[3072]{0:T(1024)} %param.26) | copy-start | bytes 36868
  0.8 6.8 %copy-start.3 = (f32[3072]{0:T(1024)S(1)}, f32[3072]{0:T(1024)}, u32[]{:S(2)}) copy-start(f32[3072]{0:T(1024)} %param.27) | copy-start | bytes 36868
  0.8 6.8 %copy-start.5 = (s32[1,512]{1,0:T(1,128)S(1)}, s32[1,512]{1,0:T(1,128)}, u32[]{:S(2)}) copy-start(s32[1,512]{1,0:T(1,128)} %prow_ref.1) | copy-start | bytes 6148

commit v5 on v4

--- a/solution.py
+++ b/solution.py
@@ -111,8 +111,8 @@
     def rs_chip_rows(s, j, b):
         return remote(part.at[b, sub(j)], take.at[s, sub(j)], rsd_s.at[s, j], rsd_r.at[s, j], partner)
 
-    def rs_chip_block(s):
-        return remote(give.at[s], take.at[s], rsd_s.at[s, 0], rsd_r.at[s, 0], partner)
+    def rs_chip_give(s, j):
+        return remote(give.at[s, sub(j)], take.at[s, sub(j)], rsd_s.at[s, j], rsd_r.at[s, j], partner)
 
     def rs_ring(r, t, j):
         slot = (r % 2) * (chips - 1) + t
@@ -131,17 +131,15 @@
         rs_ring(r, t, j).start()
 
     def rs_stage(r, t):
-        rs_chip_block(t + 1).wait_recv()
-
-        def body(j, _):
+        def body(j, _):
+            rs_chip_give(t + 1, j).wait_recv()
             rs_piece(r, t, own.at[t + 1], j)
             return 0
         lax.fori_loop(0, PIECES, body, 0)
 
     def rs_last(r, finish):
-        rs_chip_block(0).wait_recv()
-
-        def body(j, _):
+        def body(j, _):
+            rs_chip_give(0, j).wait_recv()
             finish(j, rs_sum(r, chips - 1, j, own.at[0]))
             return 0
         lax.fori_loop(0, PIECES, body, 0)
@@ -154,8 +152,11 @@
         lax.fori_loop(0, PIECES, body, 0)
 
     def block_drain():
-        for s in range(chips):
-            rs_chip_block(s).wait_send()
+        def body(j, _):
+            for s in range(chips):
+                rs_chip_give(s, j).wait_send()
+            return 0
+        lax.fori_loop(0, PIECES, body, 0)
 
     seq_len = prow_ref.shape[1]
     table_rows = seq_len // ((chips - 2) * PIECES)
@@ -255,7 +256,8 @@
         res = jnp.dot(lhs_ref[...], w_ref[...], preferred_element_type=F32).astype(BF16)
         give[s] = res[rows:]
         own[s] = res[:rows]
-        rs_chip_block(s).start()
+        for j in range(PIECES):
+            rs_chip_give(s, j).start()
 
     w_copies[n_qkv].wait()
     for i in range(chips):
@@ -294,14 +296,13 @@
         ag_join(acts2, s)
         if s == chips - 2:
             rs_stage(2, 0)
-        if s == chips - 1:
-            rs_chip_block(chips - 2).wait_recv()
         for i in range(n_tiles):
             gate_up(s, i)
             for j in range(i * per_tile, (i + 1) * per_tile):
                 if s < chips - 1:
                     ag_forward(acts2, s + 1, j)
                 else:
+                    rs_chip_give(chips - 2, j).wait_recv()
                     rs_piece(2, chips - 3, own.at[chips - 2], j)
         spread(s, h_buf, wd)
     rs_stage(2, chips - 2)
@@ -337,28 +338,28 @@
         inside = (local >= 0) & (local < vocab)
         wants.append(jnp.where(inside, place * unit + (local & 7), -1))
         hits = jnp.where((lane == place) & inside, local.astype(F32), 0.0)
-        list_v[g : g + 1, :] = jnp.sum(hits, axis=0, keepdims=True).astype(jnp.int32)
+        list_v[g, 0:1, :] = jnp.sum(hits, axis=0, keepdims=True).astype(jnp.int32)
         total = jnp.sum(row_in, axis=1, keepdims=True).astype(jnp.int32)
-        list_v[n_blocks + g : n_blocks + g + 1, :] = jnp.broadcast_to(total, (1, TOKENS))
-    to_scalars = pltpu.make_async_copy(list_v, list_s, list_sem)
-    to_scalars.start()
-    to_scalars.wait()
+        list_v[g, 1:2, :] = jnp.broadcast_to(total, (1, TOKENS))
+        pltpu.make_async_copy(list_v.at[g], list_s.at[g], list_sem.at[g]).start()
 
     for g in range(n_blocks):
+        pltpu.make_async_copy(list_v.at[g], list_s.at[g], list_sem.at[g]).wait()
+
         def issue(i, _):
-            local = list_s[g, i]
+            local = list_s[g, 0, i]
             src = pl.multiple_of(lax.shift_left(lax.shift_right_logical(local, 3), 3), unit)
             dst = pl.multiple_of((g * TOKENS + i) * unit, unit)
             pltpu.make_async_copy(table_hbm.at[pl.ds(src, unit), :], slots.at[pl.ds(dst, unit), :], sem.at[g]).start()
             return 0
-        lax.fori_loop(0, list_s[n_blocks + g, 0], issue, 0)
+        lax.fori_loop(0, list_s[g, 1, 0], issue, 0)
 
     scale = jnp.sqrt(jnp.float32(dim)).astype(BF16).astype(F32)
     col = lax.broadcasted_iota(jnp.int32, (TOKENS, depth), 1)
     slot_row = lax.broadcasted_iota(jnp.int32, (depth, dim), 0)
 
     for g in range(n_blocks):
-        count = list_s[n_blocks + g, 0]
+        count = list_s[g, 1, 0]
         want = wants[g]
 
         def wait(i, _):
@@ -392,9 +393,9 @@
         scratch_shapes=[
             pltpu.VMEM((8 * seq_len, dim), BF16),
             pltpu.VMEM((seq_len, TOKENS), jnp.int32),
-            pltpu.VMEM((2 * seq_len // TOKENS, TOKENS), jnp.int32),
-            pltpu.SMEM((2 * seq_len // TOKENS, TOKENS), jnp.int32),
-            pltpu.SemaphoreType.DMA,
+            pltpu.VMEM((seq_len // TOKENS, 8, TOKENS), jnp.int32),
+            pltpu.SMEM((seq_len // TOKENS, 8, TOKENS), jnp.int32),
+            pltpu.SemaphoreType.DMA((seq_len // TOKENS,)),
             pltpu.SemaphoreType.DMA((seq_len // TOKENS,)),
         ],
         compiler_params=pltpu.CompilerParams(vmem_limit_bytes=48 * 1024 * 1024),

time: 90.3 us -> 88.8 us (0.983)
  Pallas kernels: 88.2 us -> 87 us
    pallas_call x1, Pallas kernels: 81.4 us -> 80.2 us  [decoder_layer(): pl.pallas_call(functools.partial(layer_kernel, n_dev), name='layer', out_...]
where the time goes in v5:
time: 88.8 us; the launch traced here: 88.6 us
  Pallas kernels  87 us (98%)
  local copies, waits for them, and re-layouts  1.46 us (2%)
    pallas_call x1, Pallas kernels, decoder_layer(): pl.pallas_call(functools.partial(layer_kernel, n_dev), name='layer', out_...  80.2 us
    pallas_call x1, Pallas kernels, lookup(): pl.pallas_call(lookup_kernel, name='lookup', out_shape=jax.ShapeDtypeStru...  6.85 us

profile of v5, /device:TPU:81, one launch (start us, length us, event | category | flops | bytes accessed | tf_op | source)
XLA Modules:
  0.0 88.6 jit_solution(14759088885573927391)
XLA Ops:
  0.0 0.1 maximum_bitcast_fusion.freq_ref
  0.1 0.0 copy-start.4
  0.1 0.7 copy-done.4
  0.8 0.0 copy-start
  0.8 0.0 copy-start.1
  0.8 0.0 copy-start.2
  0.8 0.0 copy-start.3
  0.8 0.0 copy-start.5
  0.8 6.8 %lookup.1 = bf16[512,3072]{1,0:T(8,128)(2,1)S(1)} custom-call(s32[1,512]{1,0:T(1,128)S(1)} %copy-done.4, bf16[16032,3072]{1,0:T(8,128)(2,1)} %table_hbm.1), custom_call_target="tpu_custom_call" | custom-call | tf_op jit(solution)/shard_map/lookup/pallas_call | solution.py:387
  7.7 0.0 copy-done
  7.7 0.0 copy-done.1
  7.7 0.0 copy-done.2
  7.7 0.0 copy-done.3
  7.7 0.0 copy-done.5
  7.7 80.2 %layer.1 = bf16[64,3072]{1,0:T(8,128)(2,1)S(1)} custom-call(bf16[8,64,3072]{2,1,0:T(8,128)(2,1)S(1)} %bitcast.12, f32[1,128]{1,0:T(1,128)S(1)} %maximum_bitcast_fusion.freq_ref, s32[1,512]{1,0:T(1,128)S(1)} %copy-done.5, bf16[3,3072,128]{2,1,0:T(8,128)(2,1)} %bitcast.18, bf16[3072,128]{1,0:T(8,128)(2,1)} %bitcast.20, bf16[3072,128]{1,0:T(8,128)(2,1)} %bitcast.21, ...), custom_call_target="tpu_custom_call" | custom-call | tf_op jit(solution)/shard_map/layer/pallas_call | solution.py:421
  87.9 0.7 copy.16
  (1 shorter events, 0.0 us)
Async XLA Ops:
  0.1 0.7 copy-start.4
  0.8 6.9 %copy-start = (f32[3072]{0:T(1024)S(1)}, f32[3072]{0:T(1024)}, u32[]{:S(2)}) copy-start(f32[3072]{0:T(1024)} %param.24) | copy-start | bytes 36868
  0.8 6.9 %copy-start.1 = (f32[3072]{0:T(1024)S(1)}, f32[3072]{0:T(1024)}, u32[]{:S(2)}) copy-start(f32[3072]{0:T(1024)} %param.25) | copy-start | bytes 36868
  0.8 6.9 %copy-start.2 = (f32[3072]{0:T(1024)S(1)}, f32[3072]{0:T(1024)}, u32[]{:S(2)}) copy-start(f32[3072]{0:T(1024)} %param.26) | copy-start | bytes 36868
  0.8 6.9 %copy-start.3 = (f32[3072]{0:T(1024)S(1)}, f32[3072]{0:T(1024)}, u32[]{:S(2)}) copy-start(f32[3072]{0:T(1024)} %param.27) | copy-start | bytes 36868
  0.8 6.9 %copy-start.5 = (s32[1,512]{1,0:T(1,128)S(1)}, s32[1,512]{1,0:T(1,128)}, u32[]{:S(2)}) copy-start(s32[1,512]{1,0:T(1,128)} %prow_ref.1) | copy-start | bytes 6148
